TPU v7x, 128 devices: a whole 4x4x4 slice. The times are simulated.
128 devices in a mesh: dp: 8 (over x, z_hi), cls: 16 (over z_lo, y, core).
Axes of the slice: x: 4, y: 4, z: 4 (z_hi: 2, z_lo: 2; z = z_hi * 2 + z_lo), core: 2. Of those that a mesh axis runs over, the one named last changes fastest.
Arguments:
- sketches: bfloat16 [32768, 4096], P(('dp', 'cls')), may hold values from -6 to 6
- labels: int32 [32768], P(('dp', 'cls')), may hold values from 0 to 15, as said below
- places: int32 [32768], P(('dp', 'cls')), may hold values from 0 to 4095, as said below
- counts: int32 [16, 8, 128], P('cls'), may hold values from 0 to 4, as said below
- chosen: int32 [3, 16], P(None, 'cls'), may hold values from 0 to 4095, as said below
Outputs:
- gain_scores: float32 [3, 16, 4096], P(None, 'cls', 'dp')
- coverage: float32 [16, 4096], P('cls', 'dp')
Inputs may be any that keep to these rules, and one draw needn't show every extreme that they name: `labels`: every class has 8 or more examples. `places`: an example of device s (its index along dp and cls together) with class k has place m * 512 + s * 4 + j in class k's block: m is the member of dp that receives it, and for each k, m and s the j run over 0 to counts[k, m, s] - 1 without gaps, so no two examples share a place. In every draw one class and member receive 4 examples from every device. counts[k, m, s] is the number of examples of device s that take places of class k on member m. chosen[t, k] is a place of class k's block that holds an example; the 3 picks of a class differ.
All inputs are finite; a program needn't handle non-finite values.
Results may differ from a plain program's by a relative error of at most 0.0003.
Values may be sent and summed in bfloat16 or wider, within the bound.
A program may use at most 128 MiB of HBM per device.

v0:
```python
import jax
import jax.numpy as jnp
from jax import lax
from jax.sharding import PartitionSpec as P


def in_blocks(value, dim, peers):
    dims = value.shape
    blocks = value.reshape(*dims[:dim], peers, dims[dim] // peers, *dims[dim + 1 :])
    return jnp.moveaxis(blocks, dim, 0)


def laid_out(blocks, dim):
    blocks = jnp.moveaxis(blocks, 0, dim)
    dims = blocks.shape
    return blocks.reshape(*dims[:dim], dims[dim] * dims[dim + 1], *dims[dim + 2 :])


def exchange_both(value, axis, axes, splits, concats):
    sizes = [lax.axis_size(a) for a in axes]
    blocks = in_blocks(value, splits[0], sizes[0])
    blocks = jnp.moveaxis(in_blocks(blocks, splits[1] + 1, sizes[1]), 0, 1)
    inside = blocks.shape[2:]
    blocks = blocks.reshape(-1, *inside)
    blocks = lax.all_to_all(blocks, axis, split_axis=0, concat_axis=0, tiled=True)
    blocks = laid_out(blocks.reshape(*sizes, *inside), concats[0] + 1)
    return laid_out(blocks, concats[1])


def from_everyone(value, axis):
    copies = jnp.broadcast_to(value, (lax.axis_size(axis), *value.shape))
    return lax.all_to_all(copies, axis, split_axis=0, concat_axis=0, tiled=True)


def over_copies(value, axis):
    return from_everyone(value, axis).max(axis=0)


def sum_at_owner(value, axis, dim):
    peers = lax.axis_size(axis)
    blocks = lax.all_to_all(in_blocks(value, dim, peers), axis, 0, 0, tiled=True)
    return jnp.sum(blocks, axis=0)


def squared_norms(matrix):
    wide = matrix.astype(jnp.float32)
    return jnp.sum(wide * wide, axis=1)


def distances(left, left_norms, right, right_norms, width):
    inner = lax.dot_general(
        left, right, (((1,), (1,)), ((), ())), preferred_element_type=jnp.float32
    )
    return (left_norms[:, None] + right_norms[None, :] - 2.0 * inner) / width


def coverage_chain(similar_picks):
    current = jnp.zeros((similar_picks.shape[0],), jnp.float32)
    before = []
    for turn_index in range(similar_picks.shape[1]):
        before.append(current)
        current = jnp.maximum(current, similar_picks[:, turn_index])
    return (jnp.stack(before, axis=1), current)


def column_gains(similar, row_weight, row_cover):
    return jnp.stack(
        [
            jnp.sum(
                row_weight[:, None] * jnp.maximum(similar - row_cover[:, turn_index][:, None], 0.0),
                axis=0,
            )
            for turn_index in range(row_cover.shape[1])
        ]
    )


def masked_largest(pair_block, row_weight, column_weight):
    return jnp.max(jnp.where(row_weight[:, None] * column_weight[None, :] > 0.0, pair_block, 0.0))


def body(sketches, labels, places, counts, chosen):
    row_count, width = sketches.shape
    members = lax.axis_size("dp")
    owners = lax.axis_size("cls")
    devices = members * owners
    per_source = 2 * row_count // devices
    capacity = devices * per_source
    member = lax.axis_index("dp")
    picked = chosen[:, 0]
    pick_count = picked.shape[0]
    target = (places // capacity * owners + labels) * per_source + places % per_source
    send_table = (
        lax.broadcasted_iota(jnp.int32, (2 * row_count, row_count), 0) == target[None, :]
    ).astype(jnp.bfloat16)
    outgoing = jnp.dot(send_table, sketches, preferred_element_type=jnp.float32).astype(
        jnp.bfloat16
    )
    arrived = exchange_both(
        outgoing.reshape(members, owners, per_source, width),
        ("dp", "cls"),
        ("dp", "cls"),
        (0, 1),
        (0, 1),
    )
    local_rows = arrived.reshape(capacity, width)
    class_counts = counts[0]
    valid_all = (
        (
            lax.broadcasted_iota(jnp.int32, (members, devices, per_source), 2)
            < class_counts[:, :, None]
        )
        .reshape(members, capacity)
        .astype(jnp.float32)
    )
    own_valid = lax.dynamic_index_in_dim(valid_all, member, 0, keepdims=False)
    total = jnp.sum(class_counts).astype(jnp.float32)
    local_norms = squared_norms(local_rows)
    block_rows = lax.all_gather(local_rows, "dp", axis=0, tiled=True)
    spread_all = distances(local_rows, local_norms, block_rows, squared_norms(block_rows), width)
    largest = masked_largest(spread_all, own_valid, valid_all.reshape(-1))
    bound = over_copies(largest, "dp")
    similar = bound - spread_all
    pick_columns = jnp.stack(
        [
            lax.dynamic_index_in_dim(similar, picked[turn_index], 1, keepdims=False)
            for turn_index in range(pick_count)
        ],
        axis=1,
    )
    cover_before, cover_final = coverage_chain(pick_columns)
    partial_value = column_gains(similar, own_valid, cover_before)
    summed = sum_at_owner(partial_value, "dp", 1)
    gain_scores = (summed * own_valid[None, :] / total)[:, None, :]
    coverage = (cover_final * own_valid)[None, :]
    return (gain_scores, coverage)


def solution(mesh):
    placed = (
        P(("dp", "cls"), None),
        P(("dp", "cls")),
        P(("dp", "cls")),
        P("cls", None, None),
        P(None, "cls"),
    )
    return jax.shard_map(
        body,
        mesh=mesh,
        in_specs=placed,
        out_specs=(P(None, "cls", "dp"), P("cls", "dp")),
        check_vma=False,
    )
```

profile of v0, /device:TPU:9, one launch (start us, length us, event | category | flops | bytes accessed | tf_op | source)
XLA Modules:
  0.0 501.7 jit_solution(2520177475090422252)
XLA Ops:
  7.2 0.8 fusion.3
  8.1 0.7 copy-done
  8.8 3.2 convolution_convert_fusion
  12.0 7.2 %reshape_transpose_transpose_reshape_reshape_reshape.3 = bf16[128,1,1,4,4096]{4,3,0,2,1:T(4,128)(2,1)} reshape(bf16[512,4096]{1,0:T(8,128)(2,1)} %convolution_convert_fusion) | data formatting | bytes 8388608 | tf_op jit(solution)/shard_map/reshape;transpose;transpose;reshape;reshape;reshape | solution.py:24
  19.2 62.3 %all_to_all.16 = bf16[128,1,1,4,4096]{4,3,2,1,0:T(4,128)(2,1)} all-to-all(bf16[128,1,1,4,4096]{4,3,2,1,0:T(4,128)(2,1)} %bitcast.30), channel_id=1, replica_groups=mesh['dp'=8,'cls'=16] {'dp','cls'}, dimensions={0} | all-to-all | bytes 8388608 | tf_op jit(solution)/shard_map/all_to_all | solution.py:25
  81.5 6.9 %reshape_reshape.3 = bf16[512,4096]{1,0:T(8,128)(2,1)} reshape(bf16[8,16,1,4,4096]{4,3,1,0,2:T(4,128)(2,1)} %bitcast.28) | data formatting | bytes 8388608 | tf_op jit(solution)/shard_map/reshape;reshape | solution.py:106
  88.5 0.6 fusion.4
  92.8 0.7 reduce_sum.72
  97.0 5.6 %multiply_reduce_fusion.4 = f32[8,16,4]{2,1,0:T(8,128)S(1)} fusion(bf16[8,16,1,4,4096]{4,3,1,0,2:T(4,128)(2,1)} %bitcast.29), kind=kLoop, calls=%fused_computation.6 | loop fusion | flops 6290944 | bytes 4196352 | tf_op jit(solution)/shard_map/reduce_sum | solution.py:47
  102.7 323.3 %all-gather.2.cloned.1.call-done = bf16[4096,4096]{1,0:T(8,128)(2,1)} async-done(((bf16[512,4096]{1,0:T(8,128)(2,1)}), bf16[4096,4096]{1,0:T(8,128)(2,1)}) %all-gather.2.cloned.1.call-update) | async-done | bytes 33554448 | tf_op jit(solution)/shard_map/all_gather | solution.py:119
  426.0 11.5 %multiply_reduce_fusion = f32[4096]{0:T(1024)S(1)} fusion(bf16[4096,4096]{1,0:T(8,128)(2,1)} %all-gather.2.cloned.1.call-done), kind=kLoop, calls=%fused_computation | loop fusion | flops 50327552 | bytes 33570816 | tf_op jit(solution)/shard_map/reduce_sum | solution.py:47
  437.8 24.8 %select_reduce_fusion = (f32[]{:T(128)}, f32[512,4096]{1,0:T(8,128)}) fusion(f32[4096]{0:T(1024)S(1)} %compare_convert_fusion, f32[512]{0:T(512)S(1)} %get-tuple-element.17, bf16[512,4096]{1,0:T(8,128)(2,1)S(1)} %copy-done.3, bf16[4096,4096]{1,0:T(8,128)(2,1)} %all-gather.2.cloned.1.call-done, f32[4096]{0:T(1024)S(1)} %multiply_reduce_fusion, f32[512]{0:T(512)S(1)} %add.46), kind=kOutput, calls=%fused_computation.4 | convolution fusion | flops 17196646400 | bytes 46174212 | tf_op jit(solution)/shard_map/dot_general | solution.py:51
  462.6 0.6 broadcast_in_dim.5
  463.2 8.9 %all_to_all.17 = f32[8,1,1]{2,1,0:T(1,128)S(1)} all-to-all(f32[8,1,1]{2,1,0:T(1,128)S(1)} %broadcast_in_dim.5), channel_id=1, replica_groups=mesh['dp'=8,'cls'=16] {'dp'}, dimensions={0} | all-to-all | bytes 64 | tf_op jit(solution)/shard_map/all_to_all | solution.py:32
  472.1 0.6 reduce_max.19
  472.7 5.1 %broadcast_subtract_fusion = f32[512,4096]{1,0:T(8,128)S(1)} fusion(f32[512,4096]{1,0:T(8,128)} %get-tuple-element.23, f32[]{:T(128)} %reduce_max.19), kind=kLoop, calls=%fused_computation.9 | loop fusion | flops 2097152 | bytes 16777220 | tf_op jit(solution)/shard_map/sub | solution.py:123
  477.9 0.4 fusion.1
  478.5 5.1 %multiply_reduce_fusion.3 = (f32[4096]{0:T(1024)S(1)}, f32[4096]{0:T(1024)S(1)}, f32[4096]{0:T(1024)S(1)}) fusion(f32[512]{0:T(512)S(1)} %get-tuple-element.17, f32[512]{0:T(512)S(1)} %get-tuple-element.16, f32[512]{0:T(512)S(1)} %get-tuple-element.15, f32[512,4096]{1,0:T(8,128)S(1)} %copy-done.2, f32[]{:T(128)} %reduce_max.19), kind=kLoop, calls=%fused_computation.3 | loop fusion | flops 25153536 | bytes 8443908 | tf_op jit(solution)/shard_map/reduce_sum | solution.py:69
  483.6 0.7 maximum_bitcast_fusion
  484.3 3.3 all-to-all-start.2
  487.6 1.4 convert_multiply_fusion
  489.0 0.7 copy.29
  489.7 4.4 all-to-all-done.2
  494.2 0.6 multiply_divide_fusion
  (27 shorter events, 1.8 us)
Async XLA Ops:
  7.2 1.6 copy-start
  7.2 418.8 %all-gather.2.cloned.1.call-start = ((), (), s32[]{:S(2)}) async-start(), calls=%async_computation.3 | async-start | bytes 37748736 | tf_op jit(solution)/shard_map/all_gather | solution.py:119
  81.5 7.0 %copy-start.6 = (s32[3,1]{0,1:T(1,128)S(1)}, s32[3,1]{0,1:T(1,128)}, u32[]{:S(2)}) copy-start(s32[3,1]{0,1:T(1,128)} %param.9) | copy-start | bytes 40
  81.5 11.3 %copy-start.5 = (s32[1,8,128]{2,1,0:T(8,128)S(1)}, s32[1,8,128]{2,1,0:T(8,128)}, u32[]{:S(2)}) copy-start(s32[1,8,128]{2,1,0:T(8,128)} %param.8) | copy-start | bytes 12292
  426.0 11.8 %copy-start.3 = (bf16[512,4096]{1,0:T(8,128)(2,1)S(1)}, bf16[512,4096]{1,0:T(8,128)(2,1)}, u32[]{:S(2)}) copy-start(bf16[512,4096]{1,0:T(8,128)(2,1)} %reshape_reshape.3) | copy-start | bytes 12582916
  472.7 5.8 %copy-start.2 = (f32[512,4096]{1,0:T(8,128)S(1)}, f32[512,4096]{1,0:T(8,128)}, u32[]{:S(2)}) copy-start(f32[512,4096]{1,0:T(8,128)} %get-tuple-element.23) | copy-start | bytes 25165828
  472.7 22.1 %copy-start.1 = (bf16[256,4096]{1,0:T(8,128)(2,1)S(1)}, bf16[256,4096]{1,0:T(8,128)(2,1)}, u32[]{:S(2)}) copy-start(bf16[256,4096]{1,0:T(8,128)(2,1)} %param.5) | copy-start | bytes 6291460
  477.9 5.7 %copy-start.4 = (f32[512,4096]{1,0:T(8,128)}, f32[512,4096]{1,0:T(8,128)S(1)}, u32[]{:S(2)}) copy-start(f32[512,4096]{1,0:T(8,128)S(1)} %broadcast_subtract_fusion) | copy-start | bytes 25165828
  484.3 9.9 %all-to-all-start.2 = ((f32[8,3,512]{2,1,0:T(4,128)}), f32[8,3,512]{2,1,0:T(4,128)S(1)}, u32[]{:S(2)}, u32[]{:S(2)}) async-start(f32[8,3,512]{2,1,0:T(4,128)} %maximum_bitcast_fusion), calls=%async_computation.2 | async-start | bytes 131072 | tf_op jit(solution)/shard_map/all_to_all | solution.py:41
Sparse Core Ops, SparseCore 0:
  88.6 337.3 all-gather.1
where the time goes:
time: 506 us; the launch traced here: 502 us
  waiting for transfers between devices  328 us (65%)
  blocking collectives  71.2 us (14%)
  other arithmetic  32.7 us (6%)
  matrix products  28 us (6%)
  between operations  20.4 us (4%)
  local copies, waits for them, and re-layouts  18.2 us (4%)
    all_gather x1, waiting for transfers between devices, body(): block_rows = lax.all_gather(local_rows, 'dp', axis=0, tiled=True)  323 us
    all_to_all x1, blocking collectives, exchange_both(): lax.all_to_all(blocks, axis, split_axis=0, concat_axis=0, tiled=True)  62.3 us
    dot_general x1, matrix products, distances(): lax.dot_general(left, right, (((1,), (1,)), ((), ())), preferred_element_...  24.8 us
    reduce_sum x2, other arithmetic, squared_norms(): return jnp.sum(wide * wide, axis=1)  17 us
  transfers between devices with their start and end apart: 2, of which 2 were waited for; matrix products, arithmetic and copies ran while one was open for 2% of the time, Pallas kernels for 0%

commit v1 on v0

v1 whole, which is shorter than its diff:
```python
import jax
import jax.numpy as jnp
from jax import lax
from jax.experimental import pallas as pl
from jax.experimental.pallas import tpu as pltpu
from jax.sharding import PartitionSpec as P

MESH = pl.DeviceIdType.MESH
D = 4096
BIG = 1e30
PARTS = ((0, 1408), (1408, 1408), (2816, 1280))
UNIT = 32
BS = 512
NB = 8
EXT = 16
TASKS = 18


def my_coords():
    dp = lax.axis_index("dp")
    cls = lax.axis_index("cls")
    return dp // 2, (cls // 2) % 4, (dp % 2) * 2 + cls // 8, cls % 2


def device_at(x, y, z, core):
    return (x * 2 + z // 2, ((z % 2) * 4 + y) * 2 + core)


def class_at(y, z):
    return (z % 2) * 8 + y * 2 + z // 2


def plane(part, x, y, z, a, b):
    if part == 0:
        ty, tz = (y + a) % 4, (z + b) % 4
        return (x, ty, tz), class_at(ty, tz)
    if part == 1:
        tx, tz = (x + a) % 4, (z + b) % 4
        return (tx, y, tz), class_at((tx - tz + 4) % 4, tz)
    tx, ty = (x + a) % 4, (y + b) % 4
    return (tx, ty, z), class_at(ty, (tx - ty + 4) % 4)


def exchange_kernel(out_ref, vrow_ref, pick_ref, block_ref, vpart_ref, ppart_ref, relay0, relay1, relay2,
                    send1, recv1, send2, recv2, dsend, drecv, asend, arecv):
    x, y, z, core = my_coords()
    owner_x = (y + z) % 4
    owner_y = (x - z + 4) % 4
    owner_z = (x - y + 4) % 4
    is_owner = x == owner_x
    relays = (relay0, relay1, relay2)
    partner = device_at(x, y, z, 1 - core)

    aux = (
        pltpu.make_async_remote_copy(vrow_ref, vpart_ref, asend.at[0], arecv.at[0], device_id=partner, device_id_type=MESH),
        pltpu.make_async_remote_copy(pick_ref, ppart_ref, asend.at[1], arecv.at[1], device_id=partner, device_id_type=MESH),
    )
    for copy in aux:
        copy.start()

    order = [(a, b) for a in range(4) for b in range(4)]
    first = []
    for i, (a, b) in enumerate(order):
        for part, (start, size) in enumerate(PARTS):
            if (a, b) == (0, 0):
                continue
            (tx, ty, tz), klass = plane(part, x, y, z, a, b)
            copy = pltpu.make_async_remote_copy(
                out_ref.at[pl.ds(pl.multiple_of(klass * UNIT, UNIT), UNIT), pl.ds(start, size)],
                relays[part].at[i],
                send1.at[part, i],
                recv1.at[part, i],
                device_id=device_at(tx, ty, tz, core),
                device_id_type=MESH,
            )
            copy.start()
            first.append((part, i, copy))

    def forward(part, i, a, b, source):
        start, size = PARTS[part]
        if part == 0:
            sx, sy, sz = x, (y - a + 4) % 4, (z - b + 4) % 4
            target, d = (owner_x, y, z), (x - owner_x + 4) % 4
        elif part == 1:
            sx, sy, sz = (x - a + 4) % 4, y, (z - b + 4) % 4
            target, d = (x, owner_y, z), (y - owner_y + 4) % 4
        else:
            sx, sy, sz = (x - a + 4) % 4, (y - b + 4) % 4, z
            target, d = (x, y, owner_z), (z - owner_z + 4) % 4
        dest = block_ref.at[core, sx, sz, sy, :, pl.ds(start, size)]
        there = pltpu.make_async_remote_copy(
            source, dest, send2.at[part, i], recv2.at[part, d],
            device_id=device_at(*target, core), device_id_type=MESH,
        )
        here = pltpu.make_async_copy(source, dest, send2.at[part, i])
        return there, here

    second = []
    for i, (a, b) in enumerate(order):
        for part, (start, size) in enumerate(PARTS):
            if (a, b) == (0, 0):
                _, klass = plane(part, x, y, z, 0, 0)
                source = out_ref.at[pl.ds(pl.multiple_of(klass * UNIT, UNIT), UNIT), pl.ds(start, size)]
            else:
                source = relays[part].at[i]
                for p, n, copy in first:
                    if (p, n) == (part, i):
                        copy.wait_recv()
            there, here = forward(part, i, a, b, source)

            @pl.when(jnp.logical_not(is_owner))
            def _():
                there.start()

            @pl.when(is_owner)
            def _():
                here.start()

            second.append((there, here))

    def region(part, n, half):
        start, size = PARTS[part]
        if part == 0:
            return block_ref.at[half, n, :, :, :, pl.ds(start, size)]
        if part == 1:
            return block_ref.at[half, :, :, n, :, pl.ds(start, size)]
        return block_ref.at[half, :, n, :, :, pl.ds(start, size)]

    @pl.when(jnp.logical_not(is_owner))
    def _():
        for there, _ in second:
            there.wait_send()

    @pl.when(is_owner)
    def _():
        for _, here in second:
            here.wait()
        across = []
        for d in range(4):
            for part in range(3):
                n = ((x, y, z)[part] + d) % 4
                piece = region(part, n, core)
                if d:
                    pltpu.make_async_copy(piece, piece, recv2.at[part, d]).wait()
                copy = pltpu.make_async_remote_copy(
                    piece, piece, dsend.at[part, d], drecv.at[part, d], device_id=partner, device_id_type=MESH
                )
                copy.start()
                across.append(copy)
        for copy in across:
            copy.wait()

    for _, _, copy in first:
        copy.wait_send()
    for copy in aux:
        copy.wait()


def exchange(outgoing, vrow, pick):
    anywhere = pl.BlockSpec(memory_space=pl.ANY)
    vmem = pl.BlockSpec(memory_space=pltpu.VMEM)
    block, vpart, ppart = pl.pallas_call(
        exchange_kernel,
        out_shape=(
            jax.ShapeDtypeStruct((2, 4, 4, 4, UNIT, D), jnp.bfloat16),
            jax.ShapeDtypeStruct(vrow.shape, vrow.dtype),
            jax.ShapeDtypeStruct(pick.shape, pick.dtype),
        ),
        in_specs=[vmem, vmem, vmem],
        out_specs=(anywhere, vmem, vmem),
        scratch_shapes=[pltpu.VMEM((16, UNIT, size), jnp.bfloat16) for _, size in PARTS]
        + [
            pltpu.SemaphoreType.DMA((3, 16)),
            pltpu.SemaphoreType.DMA((3, 16)),
            pltpu.SemaphoreType.DMA((3, 16)),
            pltpu.SemaphoreType.DMA((3, 4)),
            pltpu.SemaphoreType.DMA((3, 4)),
            pltpu.SemaphoreType.DMA((3, 4)),
            pltpu.SemaphoreType.DMA((2,)),
            pltpu.SemaphoreType.DMA((2,)),
        ],
        compiler_params=pltpu.CompilerParams(has_side_effects=True),
        name="exchange",
    )(outgoing, vrow, pick)
    return block.reshape(NB, BS, D), vpart, ppart


def column(row):
    return jnp.broadcast_to(row, (128, row.shape[1])).T


def score_kernel(pick_ref, block_ref, valid_ref, res_ref, xs, gram, hcol, a1col, a2col, r1, r2, rg, rows, sums, peak,
                 pbuf, sems, psem):
    dp = lax.axis_index("dp")
    cls = lax.axis_index("cls")
    x, y, z = dp // 2, (cls // 2) % 4, (dp % 2) * 2 + cls // 8
    core = cls % 2
    res_ref[...] = jnp.zeros_like(res_ref)

    @pl.when(x == (y + z) % 4)
    def _():
        loads = [
            pltpu.make_async_copy(block_ref.at[b], xs.at[b, pl.ds(0, BS)], sems.at[b]) for b in range(NB)
        ]
        for t in range(3):
            c = pick_ref[0, t]
            pltpu.make_async_copy(
                block_ref.at[c // BS, pl.ds(pl.multiple_of(c % BS // 16 * 16, 16), 16)], pbuf.at[t], psem.at[t]
            ).start()
        for copy in loads:
            copy.start()
        picked = jnp.zeros((EXT, D), jnp.float32)
        line = lax.broadcasted_iota(jnp.int32, (EXT, D), 0)
        hp = []
        for t in range(3):
            c = pick_ref[0, t]
            pltpu.make_async_copy(pbuf.at[t], pbuf.at[t], psem.at[t]).wait()
            wide = pbuf[t].astype(jnp.float32)
            one = jnp.sum(jnp.where(line == c % 16, wide, 0.0), axis=0, keepdims=True)
            hp.append(0.5 * jnp.sum(one * one, axis=1, keepdims=True))
            picked = jnp.where(line == t, one, picked)
        picked = picked.astype(jnp.bfloat16)
        r1[...] = jnp.zeros_like(r1)
        r2[...] = jnp.zeros_like(r2)
        rg[...] = jnp.zeros_like(rg)
        sums[...] = jnp.zeros_like(sums)
        peak[...] = jnp.zeros_like(peak)

        def norms(b, carry):
            pltpu.make_async_copy(block_ref.at[b], xs.at[b, pl.ds(0, BS)], sems.at[b]).wait()
            xs[b, pl.ds(BS, EXT)] = picked

            def strip(i, c):
                wide = xs[b, pl.ds(pl.multiple_of(i * 32, 32), 32)].astype(jnp.float32)
                h = 0.5 * jnp.sum(wide * wide, axis=1, keepdims=True)
                hcol[b, pl.ds(pl.multiple_of(i * 32, 32), 32)] = jnp.broadcast_to(h, (32, 128))
                return c

            lax.fori_loop(0, BS // 32, strip, 0)
            hrow = hcol[b].T[0:1]
            good = valid_ref[b] > 0.0
            own = b // 4 == core
            res_ref[4, b] = jnp.where(own, hrow, 0.0)[0]
            rows[b, 0:1] = jnp.where(good[0:1], hrow, -BIG)
            hcol[b] = column(rows[b, 0:1])
            return carry

        lax.fori_loop(0, NB, norms, 0)

        def task(n, carry):
            is_diag = n < 4
            pair = n - 4
            inner_i = jnp.where(pair < 3, 0, jnp.where(pair < 5, 1, 2))
            inner_j = jnp.where(pair < 3, pair + 1, jnp.where(pair < 5, pair - 1, 3))
            cross = n - 10
            ci = jnp.where(core == 0, cross % 4, 6 + cross % 2)
            cj = jnp.where(core == 0, 4 + cross // 4, cross // 2)
            i = jnp.where(is_diag, 4 * core + n, jnp.where(n < 10, 4 * core + inner_i, ci))
            j = jnp.where(is_diag, 4 * core + n, jnp.where(n < 10, 4 * core + inner_j, cj))
            gram[...] = lax.dot_general(
                xs[i], xs[j, pl.ds(0, BS)], (((1,), (1,)), ((), ())), preferred_element_type=jnp.float32
            )
            near = gram[pl.ds(BS, 8)]
            good = valid_ref[j][0:1] > 0.0
            p1 = hp[0] - near[0:1]
            p2 = jnp.minimum(p1, hp[1] - near[1:2])
            p3 = jnp.minimum(p2, hp[2] - near[2:3])
            a1 = jnp.where(good, p1, -BIG)
            a2 = jnp.where(good, p2, -BIG)
            rows[j, 1:2] = a1
            rows[j, 2:3] = a2

            @pl.when(is_diag)
            def _():
                a1col[j] = column(a1)
                a2col[j] = column(a2)
                res_ref[3, j] = p3[0]

            hu_all = rows[j, 0:1]

            def strip(k, c):
                base = pl.multiple_of(k * 32, 32)
                hq = hcol[i, pl.ds(base, 32)]
                a1q = a1col[i, pl.ds(base, 32)]
                a2q = a2col[i, pl.ds(base, 32)]
                off = jnp.logical_not(is_diag)
                t1 = jnp.zeros((32, 128), jnp.float32)
                t2 = t1
                tg = t1
                top = peak[...]
                for cb in range(4):
                    lanes = pl.ds(cb * 128, 128)
                    g = gram[pl.ds(base, 32), lanes]
                    e = g - rows[j, 0:1, lanes]
                    f = g - hq
                    gap = hq - e
                    top = jnp.maximum(top, jnp.maximum(jnp.maximum(gap[0:8], gap[8:16]), jnp.maximum(gap[16:24], gap[24:32])))
                    u1 = jnp.maximum(e + a1q, 0.0)
                    u2 = jnp.maximum(e + a2q, 0.0)
                    sums[j, 0, :, lanes] += (u1[0:8] + u1[8:16]) + (u1[16:24] + u1[24:32])
                    sums[j, 1, :, lanes] += (u2[0:8] + u2[8:16]) + (u2[16:24] + u2[24:32])
                    sums[j, 2, :, lanes] += (g[0:8] + g[8:16]) + (g[16:24] + g[24:32])
                    t1 += jnp.maximum(f + rows[j, 1:2, lanes], 0.0)
                    t2 += jnp.maximum(f + rows[j, 2:3, lanes], 0.0)
                    tg += g
                peak[...] = top

                @pl.when(off)
                def _():
                    r1[i, pl.ds(base, 32)] += t1
                    r2[i, pl.ds(base, 32)] += t2
                    rg[i, pl.ds(base, 32)] += tg

                return c

            lax.fori_loop(0, BS // 32, strip, 0)
            return carry

        lax.fori_loop(0, TASKS, task, 0)

        def finish(b, carry):
            for n, part in enumerate((r1, r2, rg)):
                across = jnp.sum(part[b].T, axis=0, keepdims=True)
                res_ref[n, b] = (across + jnp.sum(sums[b, n], axis=0, keepdims=True))[0]
            return carry

        lax.fori_loop(0, NB, finish, 0)
        best = jnp.max(jnp.max(peak[...], axis=0, keepdims=True), axis=1, keepdims=True)
        for b in range(NB):
            res_ref[5, b] = jnp.broadcast_to(best, (1, BS))[0]


def scores(block, valid, pick):
    return pl.pallas_call(
        score_kernel,
        out_shape=jax.ShapeDtypeStruct((8, NB, BS), jnp.float32),
        in_specs=[
            pl.BlockSpec(memory_space=pltpu.SMEM),
            pl.BlockSpec(memory_space=pl.ANY),
            pl.BlockSpec(memory_space=pltpu.VMEM),
        ],
        out_specs=pl.BlockSpec(memory_space=pltpu.VMEM),
        scratch_shapes=[
            pltpu.VMEM((NB, BS + EXT, D), jnp.bfloat16),
            pltpu.VMEM((BS + EXT, BS), jnp.float32),
            pltpu.VMEM((NB, BS, 128), jnp.float32),
            pltpu.VMEM((NB, BS, 128), jnp.float32),
            pltpu.VMEM((NB, BS, 128), jnp.float32),
            pltpu.VMEM((NB, BS, 128), jnp.float32),
            pltpu.VMEM((NB, BS, 128), jnp.float32),
            pltpu.VMEM((NB, BS, 128), jnp.float32),
            pltpu.VMEM((NB, 8, BS), jnp.float32),
            pltpu.VMEM((NB, 3, 8, BS), jnp.float32),
            pltpu.VMEM((8, 128), jnp.float32),
            pltpu.VMEM((3, EXT, D), jnp.bfloat16),
            pltpu.SemaphoreType.DMA((NB,)),
            pltpu.SemaphoreType.DMA((3,)),
        ],
        compiler_params=pltpu.CompilerParams(vmem_limit_bytes=62 * 1024 * 1024),
        name="scores",
    )(pick, block, valid)


def spread_kernel(res_ref, all_ref, send, recv):
    x, y, z, core = my_coords()
    klass = class_at(y, z)
    me = lax.axis_index("dp")
    cls = lax.axis_index("cls")
    is_owner = x == (y + z) % 4

    @pl.when(is_owner)
    def _():
        copies = []
        for m in range(8):
            local = jnp.logical_and(me == m, cls == klass)
            there = pltpu.make_async_remote_copy(
                res_ref, all_ref.at[core], send.at[m], recv.at[core], device_id=(m, klass), device_id_type=MESH
            )

            @pl.when(jnp.logical_not(local))
            def _():
                there.start()

            @pl.when(local)
            def _():
                pltpu.make_async_copy(res_ref, all_ref.at[core], recv.at[core]).start()

            copies.append((local, there))
        for local, there in copies:

            @pl.when(jnp.logical_not(local))
            def _():
                there.wait_send()

    for c in range(2):
        pltpu.make_async_copy(all_ref.at[c], all_ref.at[c], recv.at[c]).wait()


def share(res):
    vmem = pl.BlockSpec(memory_space=pltpu.VMEM)
    anywhere = pl.BlockSpec(memory_space=pl.ANY)
    return pl.pallas_call(
        spread_kernel,
        out_shape=jax.ShapeDtypeStruct((2, 8, 4096), jnp.float32),
        in_specs=[vmem],
        out_specs=anywhere,
        scratch_shapes=[pltpu.SemaphoreType.DMA((8,)), pltpu.SemaphoreType.DMA((2,))],
        compiler_params=pltpu.CompilerParams(has_side_effects=True),
        name="share",
    )(res)


def body(sketches, labels, places, counts, chosen):
    member = lax.axis_index("dp")
    row_count = sketches.shape[0]
    target = labels * UNIT + places // 512 * 4 + places % 4
    table = (lax.broadcasted_iota(jnp.int32, (512, row_count), 0) == target[None, :]).astype(jnp.bfloat16)
    outgoing = jnp.dot(table, sketches, preferred_element_type=jnp.float32).astype(jnp.bfloat16)

    class_counts = counts[0]
    picked = chosen[:, 0]
    source = picked % 512 // 4
    where = source % 2 * 2048 + source // 2 * UNIT + picked // 512 * 4 + picked % 4
    pick = jnp.zeros((8, 128), jnp.int32).at[0, :3].set(where)
    by_source = class_counts.reshape(8, 64, 2)
    valid = jnp.arange(4, dtype=jnp.int32) < jnp.transpose(by_source, (2, 1, 0))[..., None]
    valid = valid.reshape(NB, 1, BS).astype(jnp.float32)

    block, vpart, ppart = exchange(outgoing, valid, pick)
    mine = lax.axis_index("cls") % 2 == member % 2
    valid_k = jnp.where(mine, valid, vpart)
    pick_k = jnp.where(mine, pick, ppart)
    res = scores(block, valid_k, pick_k)
    both = share(res.reshape(8, 4096))

    def mine_of(rows):
        cut = lax.dynamic_index_in_dim(rows.reshape(-1, 2, 64, 8, 4), member, 3, keepdims=False)
        return jnp.transpose(cut, (0, 2, 1, 3)).reshape(-1, 512)

    total = jnp.sum(class_counts).astype(jnp.float32)
    scale = 2.0 / D
    bound = jnp.maximum(both[0, 5, 0], both[1, 5, 0]) * scale
    joined = both[0, :5] + both[1, :5]
    all_h = jnp.sum(joined[4])
    cut = mine_of(joined)
    own_counts = lax.dynamic_index_in_dim(class_counts, member, 0, keepdims=False)
    own_valid = (jnp.arange(4, dtype=jnp.int32)[None, :] < own_counts[:, None]).reshape(512)
    far = total * cut[4] + all_h - cut[2]
    gains = jnp.stack([total * bound - far * scale, cut[0] * scale, cut[1] * scale])
    gain_scores = jnp.where(own_valid[None, :], gains, 0.0) / total
    coverage = jnp.where(own_valid, jnp.maximum(bound - (cut[4] + cut[3]) * scale, 0.0), 0.0)
    return (gain_scores[:, None, :], coverage[None, :])


def solution(mesh):
    placed = (
        P(("dp", "cls"), None),
        P(("dp", "cls")),
        P(("dp", "cls")),
        P("cls", None, None),
        P(None, "cls"),
    )
    return jax.shard_map(
        body,
        mesh=mesh,
        in_specs=placed,
        out_specs=(P(None, "cls", "dp"), P("cls", "dp")),
        check_vma=False,
    )
```

time: 506 us -> 272 us (0.54)
  waiting for transfers between devices: 328 us -> 0 us
  Pallas kernels: 0 us -> 242 us
  blocking collectives: 71.2 us -> 0 us
  other arithmetic: 32.7 us -> 8.39 us
  matrix products: 28 us -> 4.89 us
  between operations: 20.4 us -> 2.74 us
  local copies, waits for them, and re-layouts: 18.2 us -> 9.55 us
    all_gather x1 -> x0, waiting for transfers between devices: 323 us -> none  [body(): block_rows = lax.all_gather(local_rows, 'dp', axis=0, tiled=True)]
    pallas_call x0 -> x3, Pallas kernels: none -> 242 us  [the longest x1 139 us: share(): pl.pallas_call(spread_kernel, out_shape=jax.ShapeDtypeStruct((2, 8, 4096)...]
    all_to_all x2 -> x0, blocking collectives: 71.2 us -> none  [the longest x1 62.3 us: exchange_both(): lax.all_to_all(blocks, axis, split_axis=0, concat_axis=0, tiled=True)]
    dot_general x2 -> x1, matrix products: 28 us -> 4.89 us  [body(): jnp.dot(table, sketches, preferred_element_type=jnp.float32)]
    reduce_sum x4 -> x1, other arithmetic: 22.1 us -> 0.65 us  [body(): all_h = jnp.sum(joined[4])]
    another operation x2 -> x3, local copies, waits for them, and re-layouts: 14.1 us -> 0.4 us  [body(): jnp.stack([total * bound - far * scale, cut[0] * scale, cut[1] * scale])]
    sub x1 -> x0, other arithmetic: 5.11 us -> none  [body(): similar = bound - spread_all]
  transfers between devices with their start and end apart: 2 -> 0, of which waited for: 2 -> 0; matrix products, arithmetic and copies ran while one was open for 2% -> 0% of each run, Pallas kernels for 0% -> 0%
where the time goes in v1:
time: 272 us; the launch traced here: 268 us
  Pallas kernels  242 us (89%)
  local copies, waits for them, and re-layouts  9.55 us (4%)
  other arithmetic  8.39 us (3%)
  matrix products  4.89 us (2%)
  between operations  2.74 us (1%)
    pallas_call x1, Pallas kernels, share(): pl.pallas_call(spread_kernel, out_shape=jax.ShapeDtypeStruct((2, 8, 4096)...  139 us
    pallas_call x1, Pallas kernels, exchange(): pl.pallas_call(exchange_kernel, out_shape=(jax.ShapeDtypeStruct((2, 4, 4,...  101 us

profile of v1, /device:TPU:9, one launch (start us, length us, event | category | flops | bytes accessed | tf_op | source)
XLA Modules:
  0.0 267.7 jit_solution(9126257280958899016)
XLA Ops:
  0.6 0.8 copy.8
  1.4 0.2 fusion
  1.7 0.9 reshape.448.vrow_ref
  2.6 0.7 fusion.9
  3.3 0.6 scatter.4.pick_ref
  3.9 0.7 fusion.8
  4.6 4.9 %convolution_convert_fusion.out_ref = bf16[512,4096]{1,0:T(8,128)(2,1)} fusion(bf16[256,4096]{1,0:T(8,128)(2,1)} %param.7, s32[256]{0:T(256)S(1)} %fusion.8), kind=kOutput, calls=%fused_computation | convolution fusion | flops 1075970048 | bytes 6292480 | tf_op jit(solution)/shard_map/dot_general | solution.py:418
  9.5 101.4 %exchange.1 = (bf16[2,4,4,4,32,4096]{5,4,3,2,1,0:T(8,128)(2,1)}, f32[8,1,512]{2,1,0:T(1,128)}, s32[8,128]{1,0:T(8,128)}) custom-call(bf16[512,4096]{1,0:T(8,128)(2,1)} %convolution_convert_fusion.out_ref, f32[8,1,512]{2,1,0:T(1,128)} %reshape.448.vrow_ref, s32[8,128]{1,0:T(8,128)} %scatter.4.pick_ref), custom_call_target="tpu_custom_call" | custom-call | tf_op jit(solution)/shard_map/exchange/pallas_call | solution.py:162
  110.9 1.3 broadcast_select_fusion
  112.2 1.3 broadcast_select_fusion.2.pick_ref
  113.5 1.6 scores.1
  115.1 1.6 copy.17
  116.8 139.1 %share.1 = f32[2,8,4096]{2,1,0:T(8,128)} custom-call(f32[8,4096]{1,0:T(8,128)} %bitcast.38), custom_call_target="tpu_custom_call" | custom-call | tf_op jit(solution)/shard_map/share/pallas_call | solution.py:402
  255.9 1.2 fusion.13
  258.4 0.6 reduce_sum.18
  259.7 1.0 slice_add_fusion
  260.7 2.7 %add.153 = f32[5,2,64,8,4]{4,3,2,1,0:T(8,128)S(1)} reshape(f32[1,5,4096]{2,1,0:T(8,128)S(1)} %slice_add_fusion) | data formatting | bytes 163840 | tf_op jit(solution)/shard_map/add | solution.py:443
  263.4 0.3 constant_dynamic-slice_fusion
  263.7 0.1 copy.12
  263.9 0.6 slice_reduce_fusion
  264.5 0.7 fusion.5
  265.5 0.1 stack.13
  266.2 0.6 fusion.2
  267.2 0.6 broadcast_select_fusion.3
  (16 shorter events, 1.2 us)
Async XLA Ops:
  9.5 101.4 %copy-start = (f32[8,1,512]{2,1,0:T(1,128)S(1)}, f32[8,1,512]{2,1,0:T(1,128)}, u32[]{:S(2)}) copy-start(f32[8,1,512]{2,1,0:T(1,128)} %reshape.448.vrow_ref) | copy-start | bytes 49156
  113.5 144.9 %copy-start.1 = (s32[1,8,128]{2,1,0:T(8,128)S(1)}, s32[1,8,128]{2,1,0:T(8,128)}, u32[]{:S(2)}) copy-start(s32[1,8,128]{2,1,0:T(8,128)} %param.10) | copy-start | bytes 12292

commit v2 on v0

v2 whole, which is shorter than its diff:
```python
import jax
import jax.numpy as jnp
from jax import lax
from jax.experimental import pallas as pl
from jax.experimental.pallas import tpu as pltpu
from jax.sharding import PartitionSpec as P

MESH = pl.DeviceIdType.MESH
D = 4096
BIG = 1e30
SCALE = 2.0 / D
PARTS = ((0, 1408), (1408, 1408), (2816, 1280))
UNIT = 32
STEPS = 16
BS = 512
HALF = 2048
EXT = 16
SKEW_Y = 1
SKEW_Z = 3


def my_coords():
    dp = lax.axis_index("dp")
    cls = lax.axis_index("cls")
    return dp // 2, (cls // 2) % 4, (dp % 2) * 2 + cls // 8, cls % 2


def device_at(x, y, z, core):
    return (x * 2 + z // 2, ((z % 2) * 4 + y) * 2 + core)


def class_at(y, z):
    return (z % 2) * 8 + y * 2 + z // 2


def both_true(a, b, c):
    return jnp.logical_and(jnp.logical_and(a, b), c)


def repeat(count, step):
    def once(n, carry):
        step(n)
        return carry

    lax.fori_loop(0, count, once, 0)


def column(row):
    return jnp.broadcast_to(row, (128, row.shape[1])).T


def fold(v):
    return (v[0:8] + v[8:16]) + (v[16:24] + v[24:32])


def kernel(pick_ref, out_ref, valid_ref, all_ref, xs, relay0, relay1, relay2, gram, tab, hcol, a1col, a2col,
           r1, r2, rg, sums, peak, part, got, final, pacc, send1, recv1, send2, rstep, dsend, drecv, tsend, trecv, msend, mrecv):
    x, y, z, core = my_coords()
    relays = (relay0, relay1, relay2)
    is_owner = x == (y + z) % 4
    partner = device_at(x, y, z, 1 - core)
    klass = class_at(y, z)

    def place_of(half, n, sx, start, size):
        return xs.at[half, n // 4, pl.ds(pl.multiple_of(n % 4 * 128 + sx * UNIT, UNIT), UNIT), pl.ds(start, size)]

    def sends(n, wait):
        oy = (y - SKEW_Y * x - n // 4 + 16) % 4
        oz = (z - SKEW_Z * x - n % 4 + 16) % 4
        ox = (oy + oz) % 4
        to = class_at(oy, oz)
        for p, (start, size) in enumerate(PARTS):
            rx, ry, rz = ((x, oy, oz), (ox, y, oz), (ox, oy, z))[p]
            own = both_true(rx == x, ry == y, rz == z)
            last = both_true(rx == ox, ry == oy, rz == oz)
            source = out_ref.at[pl.ds(pl.multiple_of(to * UNIT, UNIT), UNIT), pl.ds(start, size)]
            dest = place_of(core, n, x, start, size)
            via = pltpu.make_async_remote_copy(
                source, relays[p].at[n], send1.at[p, n], recv1.at[p, n],
                device_id=device_at(rx, ry, rz, core), device_id_type=MESH,
            )
            direct = pltpu.make_async_remote_copy(
                source, dest, send1.at[p, n], rstep.at[n],
                device_id=device_at(ox, oy, oz, core), device_id_type=MESH,
            )
            here = jnp.logical_and(own, last)
            if wait:

                @pl.when(jnp.logical_not(here))
                def _():
                    direct.wait_send()

            else:

                @pl.when(jnp.logical_not(jnp.logical_or(own, last)))
                def _():
                    via.start()

                @pl.when(jnp.logical_xor(own, last))
                def _():
                    direct.start()

                @pl.when(here)
                def _():
                    pltpu.make_async_copy(source, dest, rstep.at[n]).start()

    def forwards(n, wait):
        for p, (start, size) in enumerate(PARTS):
            if p == 0:
                oy, oz = y, z
                sx = x
            elif p == 1:
                oy, oz = (x - z + 4) % 4, z
                sx = (SKEW_Y * (y - oy - n // 4) + 16) % 4
            else:
                oy, oz = y, (x - y + 4) % 4
                sx = (SKEW_Z * (z - oz - n % 4 + 8)) % 4
            ox = (oy + oz) % 4
            sy = (oy + SKEW_Y * sx + n // 4) % 4
            sz = (oz + SKEW_Z * sx + n % 4) % 4
            mine = both_true(sx == x, sy == y, sz == z)
            copy = pltpu.make_async_remote_copy(
                relays[p].at[n], place_of(core, n, sx, start, size), send2.at[p, n], rstep.at[n],
                device_id=device_at(ox, oy, oz, core), device_id_type=MESH,
            )

            @pl.when(jnp.logical_not(mine))
            def _():
                if wait:
                    copy.wait_send()
                else:
                    pltpu.make_async_copy(relays[p].at[n], relays[p].at[n], recv1.at[p, n]).wait()
                    copy.start()

    repeat(STEPS, lambda n: sends(n, False))

    @pl.when(jnp.logical_not(is_owner))
    def _():
        repeat(STEPS, lambda n: forwards(n, False))
        repeat(STEPS, lambda n: forwards(n, True))

    def tile(half, s, r, slot):
        gram[slot] = lax.dot_general(
            xs[half, s], xs[core, r], (((1,), (1,)), ((), ())), preferred_element_type=jnp.float32
        )

    def across(r):
        return pltpu.make_async_remote_copy(
            xs.at[core, r], xs.at[core, r], dsend.at[r], drecv.at[r], device_id=partner, device_id_type=MESH
        )

    def share_copy(m):
        return pltpu.make_async_remote_copy(
            final, all_ref.at[core], msend.at[m], mrecv.at[core], device_id=(m, klass), device_id_type=MESH
        )

    @pl.when(is_owner)
    def _():
        other = 1 - core
        pacc[...] = jnp.zeros_like(pacc)

        def take(half, r):
            pacc[...] += jnp.dot(pick_ref[half, r], xs[half, r], preferred_element_type=jnp.float32)

        def round_of(r):
            for q in range(4):
                rows = xs.at[core, r, pl.ds(q * 128, 128)]
                pltpu.make_async_copy(rows, rows, rstep.at[r * 4 + q]).wait()
            across(r).start()

            take(core, r)

            def own_tile(s, carry):
                tile(core, s, r, r * (r + 1) // 2 + s)
                return carry

            lax.fori_loop(0, r + 1, own_tile, 0)

            @pl.when(r > 0)
            def _():
                across(r - 1).wait_recv()
                take(other, r - 1)

                @pl.when((r - 1) % 2 == core)
                def _():
                    tile(other, r - 1, r - 1, 16 + (r - 1) // 2)

            def cross_tile(s, carry):
                tile(other, s, r, 10 + r * (r - 1) // 2 + s)
                return carry

            lax.fori_loop(0, r, cross_tile, 0)

        repeat(4, round_of)
        across(3).wait_recv()
        take(other, 3)

        @pl.when(core == 1)
        def _():
            tile(other, 3, 3, 17)

        wide = pacc[...]
        hp = [0.5 * jnp.sum(wide[t : t + 1] * wide[t : t + 1], axis=1, keepdims=True) for t in range(3)]
        picked = wide.astype(jnp.bfloat16)

        eye = lax.broadcasted_iota(jnp.int32, (128, 128), 0) == lax.broadcasted_iota(jnp.int32, (128, 128), 1)

        def group(n, xx):
            ny = (y + SKEW_Y * xx + n // 4) % 4
            nz = (z + SKEW_Z * xx + n % 4) % 4
            return ny, nz

        lane = lax.broadcasted_iota(jnp.int32, (8, 128), 1) // UNIT

        def own_rows(r):
            near = lax.dot_general(
                picked, xs[core, r], (((1,), (1,)), ((), ())), preferred_element_type=jnp.float32
            )
            for q in range(4):
                n = r * 4 + q
                lanes = slice(q * 128, q * 128 + 128)
                sub = gram[r * (r + 3) // 2, lanes, lanes]
                h = 0.5 * jnp.sum(jnp.where(eye, sub, 0.0), axis=0, keepdims=True)
                good = jnp.zeros((8, 128), jnp.float32)
                for xx in range(4):
                    ny, nz = group(n, xx)
                    piece = jnp.broadcast_to(valid_ref[core * 16 + xx * 4 + ny], (8, 128))
                    good = jnp.where(lane == xx, pltpu.roll(piece, (xx - nz + 4) % 4 * UNIT, 1), good)
                ok = good[0:1] > 0.0
                p1 = hp[0] - near[0:1, lanes]
                p2 = jnp.minimum(p1, hp[1] - near[1:2, lanes])
                p3 = jnp.minimum(p2, hp[2] - near[2:3, lanes])
                tab[core, r, 0:1, lanes] = jnp.where(ok, h, -BIG)
                tab[core, r, 1:2, lanes] = jnp.where(ok, p1, -BIG)
                tab[core, r, 2:3, lanes] = jnp.where(ok, p2, -BIG)
                tab[core, r, 3:4, lanes] = p3
                tab[core, r, 4:5, lanes] = h
                tab[core, r, 5:6, lanes] = good[0:1]

        repeat(4, own_rows)
        sums[...] = jnp.zeros_like(sums)
        peak[...] = jnp.zeros_like(peak)
        tables = pltpu.make_async_remote_copy(
            tab.at[core], tab.at[core], tsend.at[0], trecv.at[0], device_id=partner, device_id_type=MESH
        )

        def row_block(b):
            half = jnp.where(b < 4, core, other)
            s = b % 4
            mine = b < 4

            @pl.when(b == 1)
            def _():
                tables.start()

            @pl.when(b == 4)
            def _():
                tables.wait()

            hcol[...] = column(tab[half, s, 0:1])
            a1col[...] = column(tab[half, s, 1:2])
            a2col[...] = column(tab[half, s, 2:3])
            r1[...] = jnp.zeros_like(r1)
            r2[...] = jnp.zeros_like(r2)
            rg[...] = jnp.zeros_like(rg)

            def one_tile(r, carry):
                slot = jnp.where(
                    mine, r * (r + 1) // 2 + s, jnp.where(r == s, 16 + s // 2, 10 + r * (r - 1) // 2 + s)
                )
                diag = jnp.logical_and(mine, r == s)

                def sweep(rows_too):
                    for cb in range(4):
                        lanes = slice(cb * 128, cb * 128 + 128)
                        hu = tab[core, r, 0:1, lanes]
                        a1u = tab[core, r, 1:2, lanes]
                        a2u = tab[core, r, 2:3, lanes]

                        def strip(k, acc):
                            c1, c2, cg, top = acc
                            at = pl.ds(pl.multiple_of(k * 32, 32), 32)
                            g = gram[slot, at, lanes]
                            hq = hcol[at]
                            e = g - hu
                            gap = hq - e
                            c1 = c1 + fold(jnp.maximum(e + a1col[at], 0.0))
                            c2 = c2 + fold(jnp.maximum(e + a2col[at], 0.0))
                            cg = cg + fold(g)
                            top = jnp.maximum(
                                top, jnp.maximum(jnp.maximum(gap[0:8], gap[8:16]), jnp.maximum(gap[16:24], gap[24:32]))
                            )
                            if rows_too:
                                f = g - hq
                                r1[at] += jnp.maximum(f + a1u, 0.0)
                                r2[at] += jnp.maximum(f + a2u, 0.0)
                                rg[at] += g
                            return c1, c2, cg, top

                        zero = jnp.zeros((8, 128), jnp.float32)
                        c1, c2, cg, top = lax.fori_loop(0, BS // 32, strip, (zero, zero, zero, peak[...]), unroll=4)
                        sums[r, 0, :, lanes] += c1
                        sums[r, 1, :, lanes] += c2
                        sums[r, 2, :, lanes] += cg
                        peak[...] = top

                @pl.when(diag)
                def _():
                    sweep(False)

                @pl.when(jnp.logical_not(diag))
                def _():
                    sweep(True)

                return carry

            begin = jnp.where(jnp.logical_or(mine, s % 2 == core), s, s + 1)
            lax.fori_loop(begin, 4, one_tile, 0)
            for n, acc in enumerate((r1, r2, rg)):
                part[half, s, n : n + 1] = jnp.sum(acc[...].T, axis=0, keepdims=True)

        repeat(8, row_block)
        best = jnp.max(jnp.max(peak[...], axis=0, keepdims=True), axis=1, keepdims=True)
        for r in range(4):
            part[other, r, 3:4] = jnp.broadcast_to(best, (1, BS))
        partial = pltpu.make_async_remote_copy(
            part.at[other], got, tsend.at[1], trecv.at[1], device_id=partner, device_id_type=MESH
        )
        total = jnp.sum(jnp.sum(valid_ref[...], axis=0), axis=1, keepdims=True)
        h_sum = jnp.zeros((1, 1), jnp.float32)
        for half in range(2):
            for r in range(4):
                h_sum = h_sum + jnp.sum(tab[half, r, 4:5], axis=1, keepdims=True)
        partial.start()
        partial.wait()
        bound = jnp.maximum(best, got[0, 3:4, 0:1]) * SCALE

        for r in range(4):
            cols = [jnp.sum(sums[r, n], axis=0, keepdims=True) + part[core, r, n : n + 1] + got[r, n : n + 1] for n in range(3)]
            h = tab[core, r, 4:5]
            ok = tab[core, r, 5:6] > 0.0
            far = total * h + h_sum - cols[2]
            part[core, r, 4:5] = jnp.where(ok, (total * bound - far * SCALE) / total, 0.0)
            part[core, r, 5:6] = jnp.where(ok, cols[0] * SCALE / total, 0.0)
            part[core, r, 6:7] = jnp.where(ok, cols[1] * SCALE / total, 0.0)
            part[core, r, 7:8] = jnp.where(ok, jnp.maximum(bound - (h + tab[core, r, 3:4]) * SCALE, 0.0), 0.0)

        def natural(n):
            xx, ny = n // 4, n % 4
            i1 = (ny - y - SKEW_Y * xx + 16) % 4
            piece = jnp.zeros((8, 128), jnp.float32)
            for nz in range(4):
                i2 = (nz - z - SKEW_Z * xx + 16) % 4
                take = part[core, i1, :, pl.ds(pl.multiple_of(i2 * 128, 128), 128)]
                piece = jnp.where(lane == nz, pltpu.roll(take, (nz - xx + 4) % 4 * UNIT, 1), piece)
            final[:, pl.ds(pl.multiple_of(n * 128, 128), 128)] = piece[4:8]

        repeat(16, natural)
        me = lax.axis_index("dp")
        cls = lax.axis_index("cls")
        for m in range(8):
            local = jnp.logical_and(me == m, cls == klass)

            @pl.when(jnp.logical_not(local))
            def _():
                share_copy(m).start()

            @pl.when(local)
            def _():
                all_ref[core] = final[...]

        for m in range(8):
            local = jnp.logical_and(me == m, cls == klass)

            @pl.when(jnp.logical_not(local))
            def _():
                share_copy(m).wait_send()

        repeat(4, lambda r: across(r).wait_send())

    repeat(STEPS, lambda n: sends(n, True))
    cls = lax.axis_index("cls")
    for c in range(2):
        local = both_true(is_owner, core == c, cls == klass)

        @pl.when(jnp.logical_not(local))
        def _():
            pltpu.make_async_copy(all_ref.at[c], all_ref.at[c], mrecv.at[c]).wait()


def select_facilities(outgoing, valid, pick):
    vmem = pl.BlockSpec(memory_space=pltpu.VMEM)
    sems = pltpu.SemaphoreType.DMA
    wide = pltpu.VMEM((BS, 128), jnp.float32)
    return pl.pallas_call(
        kernel,
        out_shape=jax.ShapeDtypeStruct((2, 4, HALF), jnp.float32),
        in_specs=[vmem, pl.BlockSpec(memory_space=pl.ANY), vmem],
        out_specs=vmem,
        scratch_shapes=[pltpu.VMEM((2, 4, BS, D), jnp.bfloat16)]
        + [pltpu.VMEM((STEPS, UNIT, size), jnp.bfloat16) for _, size in PARTS]
        + [
            pltpu.VMEM((18, BS, BS), jnp.float32),
            pltpu.VMEM((2, 4, 8, BS), jnp.float32),
            wide, wide, wide, wide, wide, wide,
            pltpu.VMEM((4, 3, 8, BS), jnp.float32),
            pltpu.VMEM((8, 128), jnp.float32),
            pltpu.VMEM((2, 4, 8, BS), jnp.float32),
            pltpu.VMEM((4, 8, BS), jnp.float32),
            pltpu.VMEM((4, HALF), jnp.float32),
            pltpu.VMEM((EXT, D), jnp.float32),
            sems((3, STEPS)), sems((3, STEPS)), sems((3, STEPS)), sems((STEPS,)),
            sems((4,)), sems((4,)), sems((2,)), sems((2,)), sems((8,)), sems((2,)),
        ],
        compiler_params=pltpu.CompilerParams(has_side_effects=True, vmem_limit_bytes=62 * 1024 * 1024),
        name="facilities",
    )(pick, outgoing, valid)


def body(sketches, labels, places, counts, chosen):
    member = lax.axis_index("dp")
    cls = lax.axis_index("cls")
    row_count = sketches.shape[0]
    info = jnp.concatenate([counts[0], jnp.pad(chosen[:, :1], ((0, 5), (0, 127)))], axis=0)
    swapped = lax.ppermute(info, "cls", [(n, n ^ 1) for n in range(16)])
    target = labels * UNIT + places // 512 * 4 + places % 4
    table = (lax.broadcasted_iota(jnp.int32, (512, row_count), 0) == target[None, :]).astype(jnp.bfloat16)
    outgoing = jnp.dot(table, sketches, preferred_element_type=jnp.float32).astype(jnp.bfloat16)

    x, y, z, core = member // 2, (cls // 2) % 4, (member % 2) * 2 + cls // 8, cls % 2
    info = jnp.where(core == z // 2, info, swapped)
    picked = info[8:11, 0]
    source = picked % 512 // 4
    sx, sz, sy, score = source // 32, source // 8 % 4, source // 2 % 4, source % 2
    step = (sy - y - SKEW_Y * sx + 16) % 4 * 4 + (sz - z - SKEW_Z * sx + 16) % 4
    where = score * HALF + step * 128 + sx * UNIT + picked // 512 * 4 + picked % 4
    spot = jnp.pad(where, (0, EXT - 3), constant_values=-1)
    line = jnp.arange(4096, dtype=jnp.int32).reshape(8, 1, BS)
    pick = (line == spot[None, :, None]).astype(jnp.bfloat16).reshape(2, 4, EXT, BS)
    by_source = jnp.transpose(info[:8].reshape(8, 4, 4, 4, 2), (4, 1, 3, 2, 0))
    valid = (jnp.arange(4, dtype=jnp.int32) < by_source[..., None]).astype(jnp.float32).reshape(32, 1, 128)

    both = select_facilities(outgoing, valid, pick)
    cut = lax.dynamic_index_in_dim(both.reshape(2, 4, 4, 4, 4, 8, 4), member, 5, keepdims=False)
    rows = jnp.transpose(cut, (1, 2, 4, 3, 0, 5)).reshape(4, 512)
    return (rows[:3, None, :], rows[3:4])


def solution(mesh):
    placed = (
        P(("dp", "cls"), None),
        P(("dp", "cls")),
        P(("dp", "cls")),
        P("cls", None, None),
        P(None, "cls"),
    )
    return jax.shard_map(
        body,
        mesh=mesh,
        in_specs=placed,
        out_specs=(P(None, "cls", "dp"), P("cls", "dp")),
        check_vma=False,
    )
```

time: 506 us -> 189 us (0.37)
  waiting for transfers between devices: 328 us -> 0.01 us
  Pallas kernels: 0 us -> 173 us
  blocking collectives: 71.2 us -> 0 us
  other arithmetic: 32.7 us -> 2.97 us
  matrix products: 28 us -> 4.79 us
  between operations: 20.4 us -> 0.75 us
  local copies, waits for them, and re-layouts: 18.2 us -> 6.55 us
    all_gather x1 -> x0, waiting for transfers between devices: 323 us -> none  [body(): block_rows = lax.all_gather(local_rows, 'dp', axis=0, tiled=True)]
    pallas_call x0 -> x1, Pallas kernels: none -> 173 us  [select_facilities(): pl.pallas_call(kernel, out_shape=jax.ShapeDtypeStruct((2, 4, HALF), jnp.f...]
    all_to_all x2 -> x0, blocking collectives: 71.2 us -> none  [the longest x1 62.3 us: exchange_both(): lax.all_to_all(blocks, axis, split_axis=0, concat_axis=0, tiled=True)]
    dot_general x2 -> x1, matrix products: 28 us -> 4.79 us  [body(): jnp.dot(table, sketches, preferred_element_type=jnp.float32)]
    reduce_sum x5 -> x0, other arithmetic: 22.8 us -> none  [the longest x2 17 us: squared_norms(): return jnp.sum(wide * wide, axis=1)]
    another operation x2 -> x0, local copies, waits for them, and re-layouts: 14.1 us -> none  [the longest x1 7.2 us: exchange_both(): blocks = blocks.reshape(-1, *inside)]
    sub x1 -> x0, other arithmetic: 5.11 us -> none  [body(): similar = bound - spread_all]
  transfers between devices with their start and end apart: 2 -> 1, of which waited for: 2 -> 0; matrix products, arithmetic and copies ran while one was open for 2% -> 3% of each run, Pallas kernels for 0% -> 0%
where the time goes in v2:
time: 189 us
  Pallas kernels  173 us (92%)
  local copies, waits for them, and re-layouts  6.55 us (3%)
  matrix products  4.79 us (3%)
  other arithmetic  2.97 us (2%)
    pallas_call x1, Pallas kernels, select_facilities(): pl.pallas_call(kernel, out_shape=jax.ShapeDtypeStruct((2, 4, HALF), jnp.f...  173 us
    dot_general x1, matrix products, body(): jnp.dot(table, sketches, preferred_element_type=jnp.float32)  4.79 us
  transfers between devices with their start and end apart: 1, of which 0 were waited for; matrix products, arithmetic and copies ran while one was open for 3% of the time, Pallas kernels for 0%

profile of v2, /device:TPU:9, one launch (start us, length us, event | category | flops | bytes accessed | tf_op | source)
XLA Modules:
  0.0 189.0 jit_solution(2797661702306080451)
XLA Ops:
  0.6 0.7 copy.32
  1.4 0.7 pad_add_fusion
  2.1 0.1 copy.34
  2.2 0.7 collective-permute-start
  2.9 0.7 fusion.1
  3.6 4.8 %convolution_convert_fusion.out_ref = bf16[512,4096]{1,0:T(8,128)(2,1)} fusion(bf16[256,4096]{1,0:T(8,128)(2,1)} %param.5, s32[256]{0:T(256)S(1)} %fusion.1), kind=kOutput, calls=%fused_computation | convolution fusion | flops 1075970048 | bytes 6292480 | tf_op jit(solution)/shard_map/dot_general | solution.py:428
  8.4 0.1 iota_add_fusion
  8.5 0.1 lt.90
  8.6 0.0 collective-permute-done
  8.7 0.1 fusion.3
  8.8 0.2 lt.92
  9.0 0.3 lt.93
  9.3 0.7 compare_convert_fusion.pick_ref
  10.0 0.6 compare_convert_fusion.1.valid_ref
  10.7 173.2 %facilities.1 = f32[2,4,2048]{2,1,0:T(4,128)} custom-call(bf16[2,4,16,512]{3,2,1,0:T(8,128)(2,1)} %compare_convert_fusion.pick_ref, bf16[512,4096]{1,0:T(8,128)(2,1)} %convolution_convert_fusion.out_ref, f32[32,1,128]{2,1,0:T(1,128)} %compare_convert_fusion.1.valid_ref), custom_call_target="tpu_custom_call" | custom-call | tf_op jit(solution)/shard_map/facilities/pallas_call | solution.py:395
  183.9 3.0 %reshape.82 = f32[2,4,4,4,4,8,4]{6,5,4,3,2,1,0:T(8,128)S(1)} reshape(f32[2,4,2048]{2,1,0:T(4,128)} %facilities.1) | data formatting | bytes 131072 | tf_op jit(solution)/shard_map/reshape | solution.py:444
  186.9 0.3 constant_dynamic-slice_fusion
  187.2 0.2 copy.38
  187.4 0.9 broadcast_in_dim.3
  188.3 0.1 copy.39
  188.3 0.7 slice.20
  (8 shorter events, 0.1 us)
Async XLA Ops:
  2.2 6.5 %collective-permute-start = (s32[16,128]{0,1:T(8,128)S(1)}, s32[16,128]{0,1:T(8,128)S(1)}, u32[]{:S(2)}, u32[]{:S(2)}) collective-permute-start(s32[16,128]{0,1:T(8,128)S(1)} %copy.34), channel_id=1, source_target_pairs={{0,1},{1,0},{2,3},{3,2},{4,5},{5,4},{6,7},{7,6},{8,9},{9,8},{10,11... | collective-permute-start | bytes 24584 | tf_op jit(solution)/shard_map/ppermute | solution.py:425

commit v3 on v2

--- a/solution.py
+++ b/solution.py
@@ -53,8 +53,8 @@
     return (v[0:8] + v[8:16]) + (v[16:24] + v[24:32])
 
 
-def kernel(pick_ref, out_ref, valid_ref, all_ref, xs, relay0, relay1, relay2, gram, tab, hcol, a1col, a2col,
-           r1, r2, rg, sums, peak, part, got, final, pacc, send1, recv1, send2, rstep, dsend, drecv, tsend, trecv, msend, mrecv):
+def kernel(pick_ref, out_ref, valid_ref, gain_ref, cover_ref, xs, relay0, relay1, relay2, gram, tab, hcol, a1col, a2col,
+           r1, r2, rg, sums, peak, part, got, final, pacc, landed, send1, recv1, send2, rstep, dsend, drecv, tsend, trecv, msend, mrecv):
     x, y, z, core = my_coords()
     relays = (relay0, relay1, relay2)
     is_owner = x == (y + z) % 4
@@ -63,6 +63,19 @@
 
     def place_of(half, n, sx, start, size):
         return xs.at[half, n // 4, pl.ds(pl.multiple_of(n % 4 * 128 + sx * UNIT, UNIT), UNIT), pl.ds(start, size)]
+
+    def beside(p, owner):
+        line = (owner[p] + 1 + 2 * (owner[p] % 2)) % 4
+        return line, tuple(line if q == p else owner[q] for q in range(3))
+
+    def detour(p, n, owner, source, sem):
+        _, chip = beside(p, owner)
+        slot = STEPS + n // 2
+        copy = pltpu.make_async_remote_copy(
+            source, relays[p].at[slot], sem, recv1.at[p, slot],
+            device_id=device_at(*chip, core), device_id_type=MESH,
+        )
+        return jnp.logical_and(((x, y, z)[p] - owner[p] + 4) % 4 == 2, n % 2 == 1), copy
 
     def sends(n, wait):
         oy = (y - SKEW_Y * x - n // 4 + 16) % 4
@@ -84,6 +97,8 @@
                 device_id=device_at(ox, oy, oz, core), device_id_type=MESH,
             )
             here = jnp.logical_and(own, last)
+            aside, bypass = detour(p, n, (ox, oy, oz), source, send1.at[p, n])
+            aside = jnp.logical_and(own, aside)
             if wait:
 
                 @pl.when(jnp.logical_not(here))
@@ -96,41 +111,80 @@
                 def _():
                     via.start()
 
-                @pl.when(jnp.logical_xor(own, last))
+                @pl.when(jnp.logical_and(jnp.logical_xor(own, last), jnp.logical_not(aside)))
                 def _():
                     direct.start()
 
+                @pl.when(aside)
+                def _():
+                    bypass.start()
+
                 @pl.when(here)
                 def _():
                     pltpu.make_async_copy(source, dest, rstep.at[n]).start()
 
+    def line_owner(p):
+        if p == 0:
+            return (y + z) % 4, y, z
+        if p == 1:
+            return x, (x - z + 4) % 4, z
+        return x, y, (x - y + 4) % 4
+
+    def source_of(p, n, owner, line):
+        _, oy, oz = owner
+        if p == 0:
+            sx = line
+        elif p == 1:
+            sx = (SKEW_Y * (line - oy - n // 4) + 16) % 4
+        else:
+            sx = (SKEW_Z * (line - oz - n % 4 + 8)) % 4
+        return sx, (oy + SKEW_Y * sx + n // 4) % 4, (oz + SKEW_Z * sx + n % 4) % 4
+
+    def pass_on(p, n, slot, owner, sx):
+        start, size = PARTS[p]
+        return pltpu.make_async_remote_copy(
+            relays[p].at[slot], place_of(core, n, sx, start, size), send2.at[p, slot], rstep.at[n],
+            device_id=device_at(*owner, core), device_id_type=MESH,
+        )
+
+    def arrived(p, slot):
+        pltpu.make_async_copy(relays[p].at[slot], relays[p].at[slot], recv1.at[p, slot]).wait()
+
     def forwards(n, wait):
-        for p, (start, size) in enumerate(PARTS):
-            if p == 0:
-                oy, oz = y, z
-                sx = x
-            elif p == 1:
-                oy, oz = (x - z + 4) % 4, z
-                sx = (SKEW_Y * (y - oy - n // 4) + 16) % 4
-            else:
-                oy, oz = y, (x - y + 4) % 4
-                sx = (SKEW_Z * (z - oz - n % 4 + 8)) % 4
-            ox = (oy + oz) % 4
-            sy = (oy + SKEW_Y * sx + n // 4) % 4
-            sz = (oz + SKEW_Z * sx + n % 4) % 4
+        for p in range(3):
+            owner = line_owner(p)
+            here = (x, y, z)[p]
+            sx, sy, sz = source_of(p, n, owner, here)
             mine = both_true(sx == x, sy == y, sz == z)
-            copy = pltpu.make_async_remote_copy(
-                relays[p].at[n], place_of(core, n, sx, start, size), send2.at[p, n], rstep.at[n],
-                device_id=device_at(ox, oy, oz, core), device_id_type=MESH,
-            )
+            copy = pass_on(p, n, n, owner, sx)
+            aside, bypass = detour(p, n, owner, relays[p].at[n], send2.at[p, n])
 
             @pl.when(jnp.logical_not(mine))
             def _():
                 if wait:
                     copy.wait_send()
                 else:
-                    pltpu.make_async_copy(relays[p].at[n], relays[p].at[n], recv1.at[p, n]).wait()
-                    copy.start()
+                    arrived(p, n)
+
+                    @pl.when(aside)
+                    def _():
+                        bypass.start()
+
+                    @pl.when(jnp.logical_not(aside))
+                    def _():
+                        copy.start()
+
+            slot = STEPS + n // 2
+            fx, _, _ = source_of(p, n, owner, (owner[p] + 2) % 4)
+            far = pass_on(p, n, slot, owner, fx)
+
+            @pl.when(jnp.logical_and(here == beside(p, owner)[0], n % 2 == 1))
+            def _():
+                if wait:
+                    far.wait_send()
+                else:
+                    arrived(p, slot)
+                    far.start()
 
     repeat(STEPS, lambda n: sends(n, False))
 
@@ -144,14 +198,26 @@
             xs[half, s], xs[core, r], (((1,), (1,)), ((), ())), preferred_element_type=jnp.float32
         )
 
+    def half_tile(half, s, h, slot):
+        lines = pl.ds(pl.multiple_of(h * 256, 256), 256)
+        gram[slot, :, lines] = lax.dot_general(
+            xs[half, s], xs[core, 3, lines], (((1,), (1,)), ((), ())), preferred_element_type=jnp.float32
+        )
+
     def across(r):
         return pltpu.make_async_remote_copy(
             xs.at[core, r], xs.at[core, r], dsend.at[r], drecv.at[r], device_id=partner, device_id_type=MESH
         )
 
+    def across_half(h):
+        rows = xs.at[core, 3, pl.ds(pl.multiple_of(h * 256, 256), 256)]
+        return pltpu.make_async_remote_copy(
+            rows, rows, dsend.at[3 + h], drecv.at[3 + h], device_id=partner, device_id_type=MESH
+        )
+
     def share_copy(m):
         return pltpu.make_async_remote_copy(
-            final, all_ref.at[core], msend.at[m], mrecv.at[core], device_id=(m, klass), device_id_type=MESH
+            final.at[m], landed.at[core], msend.at[m], mrecv.at[core], device_id=(m, klass), device_id_type=MESH
         )
 
     @pl.when(is_owner)
@@ -162,12 +228,22 @@
         def take(half, r):
             pacc[...] += jnp.dot(pick_ref[half, r], xs[half, r], preferred_element_type=jnp.float32)
 
+        def steps_in(r, first, count):
+            for q in range(count):
+                rows = xs.at[core, r, pl.ds(pl.multiple_of((first + q) * 128, 128), 128)]
+                pltpu.make_async_copy(rows, rows, rstep.at[r * 4 + first + q]).wait()
+
+        def other_in(r):
+            across(r).wait_recv()
+            take(other, r)
+
+            @pl.when(r % 2 == core)
+            def _():
+                tile(other, r, r, 16 + r // 2)
+
         def round_of(r):
-            for q in range(4):
-                rows = xs.at[core, r, pl.ds(q * 128, 128)]
-                pltpu.make_async_copy(rows, rows, rstep.at[r * 4 + q]).wait()
+            steps_in(r, 0, 4)
             across(r).start()
-
             take(core, r)
 
             def own_tile(s, carry):
@@ -178,12 +254,7 @@
 
             @pl.when(r > 0)
             def _():
-                across(r - 1).wait_recv()
-                take(other, r - 1)
-
-                @pl.when((r - 1) % 2 == core)
-                def _():
-                    tile(other, r - 1, r - 1, 16 + (r - 1) // 2)
+                other_in(r - 1)
 
             def cross_tile(s, carry):
                 tile(other, s, r, 10 + r * (r - 1) // 2 + s)
@@ -191,8 +262,24 @@
 
             lax.fori_loop(0, r, cross_tile, 0)
 
-        repeat(4, round_of)
-        across(3).wait_recv()
+        repeat(3, round_of)
+
+        def last_half(h):
+            steps_in(3, 2 * h, 2)
+            across_half(h).start()
+            repeat(3, lambda s: half_tile(core, s, h, 6 + s))
+
+            @pl.when(h == 0)
+            def _():
+                other_in(2)
+
+            repeat(3, lambda s: half_tile(other, s, h, 13 + s))
+
+        repeat(2, last_half)
+        take(core, 3)
+        tile(core, 3, 3, 9)
+        for h in range(2):
+            across_half(h).wait_recv()
         take(other, 3)
 
         @pl.when(core == 1)
@@ -353,8 +440,12 @@
                 i2 = (nz - z - SKEW_Z * xx + 16) % 4
                 take = part[core, i1, :, pl.ds(pl.multiple_of(i2 * 128, 128), 128)]
                 piece = jnp.where(lane == nz, pltpu.roll(take, (nz - xx + 4) % 4 * UNIT, 1), piece)
-            final[:, pl.ds(pl.multiple_of(n * 128, 128), 128)] = piece[4:8]
-
+            seat = lax.broadcasted_iota(jnp.int32, (8, 128), 1) % UNIT // 4 == 2 * ny + core
+            for m in range(8):
+                spot = pltpu.roll(piece, (2 * ny + core - m + 32) * 4 % 128, 1)
+                final[m, :, pl.ds(pl.multiple_of(xx * 128, 128), 128)] += jnp.where(seat, spot, 0.0)[4:8]
+
+        final[...] = jnp.zeros_like(final)
         repeat(16, natural)
         me = lax.axis_index("dp")
         cls = lax.axis_index("cls")
@@ -367,7 +458,7 @@
 
             @pl.when(local)
             def _():
-                all_ref[core] = final[...]
+                landed[core] = final[m]
 
         for m in range(8):
             local = jnp.logical_and(me == m, cls == klass)
@@ -376,7 +467,8 @@
             def _():
                 share_copy(m).wait_send()
 
-        repeat(4, lambda r: across(r).wait_send())
+        repeat(3, lambda r: across(r).wait_send())
+        repeat(2, lambda h: across_half(h).wait_send())
 
     repeat(STEPS, lambda n: sends(n, True))
     cls = lax.axis_index("cls")
@@ -385,7 +477,12 @@
 
         @pl.when(jnp.logical_not(local))
         def _():
-            pltpu.make_async_copy(all_ref.at[c], all_ref.at[c], mrecv.at[c]).wait()
+            pltpu.make_async_copy(landed.at[c], landed.at[c], mrecv.at[c]).wait()
+
+    rows = landed[0] + landed[1]
+    for t in range(3):
+        gain_ref[t] = rows[t : t + 1]
+    cover_ref[...] = rows[3:4]
 
 
 def select_facilities(outgoing, valid, pick):
@@ -394,11 +491,11 @@
     wide = pltpu.VMEM((BS, 128), jnp.float32)
     return pl.pallas_call(
         kernel,
-        out_shape=jax.ShapeDtypeStruct((2, 4, HALF), jnp.float32),
+        out_shape=(jax.ShapeDtypeStruct((3, 1, BS), jnp.float32), jax.ShapeDtypeStruct((1, BS), jnp.float32)),
         in_specs=[vmem, pl.BlockSpec(memory_space=pl.ANY), vmem],
-        out_specs=vmem,
+        out_specs=(vmem, vmem),
         scratch_shapes=[pltpu.VMEM((2, 4, BS, D), jnp.bfloat16)]
-        + [pltpu.VMEM((STEPS, UNIT, size), jnp.bfloat16) for _, size in PARTS]
+        + [pltpu.VMEM((STEPS + STEPS // 2, UNIT, size), jnp.bfloat16) for _, size in PARTS]
         + [
             pltpu.VMEM((18, BS, BS), jnp.float32),
             pltpu.VMEM((2, 4, 8, BS), jnp.float32),
@@ -407,10 +504,11 @@
             pltpu.VMEM((8, 128), jnp.float32),
             pltpu.VMEM((2, 4, 8, BS), jnp.float32),
             pltpu.VMEM((4, 8, BS), jnp.float32),
-            pltpu.VMEM((4, HALF), jnp.float32),
+            pltpu.VMEM((8, 4, BS), jnp.float32),
             pltpu.VMEM((EXT, D), jnp.float32),
-            sems((3, STEPS)), sems((3, STEPS)), sems((3, STEPS)), sems((STEPS,)),
-            sems((4,)), sems((4,)), sems((2,)), sems((2,)), sems((8,)), sems((2,)),
+            pltpu.VMEM((2, 4, BS), jnp.float32),
+            sems((3, STEPS)), sems((3, STEPS + STEPS // 2)), sems((3, STEPS + STEPS // 2)), sems((STEPS,)),
+            sems((5,)), sems((5,)), sems((2,)), sems((2,)), sems((8,)), sems((2,)),
         ],
         compiler_params=pltpu.CompilerParams(has_side_effects=True, vmem_limit_bytes=62 * 1024 * 1024),
         name="facilities",
@@ -440,10 +538,7 @@
     by_source = jnp.transpose(info[:8].reshape(8, 4, 4, 4, 2), (4, 1, 3, 2, 0))
     valid = (jnp.arange(4, dtype=jnp.int32) < by_source[..., None]).astype(jnp.float32).reshape(32, 1, 128)
 
-    both = select_facilities(outgoing, valid, pick)
-    cut = lax.dynamic_index_in_dim(both.reshape(2, 4, 4, 4, 4, 8, 4), member, 5, keepdims=False)
-    rows = jnp.transpose(cut, (1, 2, 4, 3, 0, 5)).reshape(4, 512)
-    return (rows[:3, None, :], rows[3:4])
+    return select_facilities(outgoing, valid, pick)
 
 
 def solution(mesh):

time: 189 us -> 174 us (0.921)
  Pallas kernels: 173 us -> 161 us
  local copies, waits for them, and re-layouts: 6.55 us -> 3.98 us
    pallas_call x1, Pallas kernels: 173 us -> 161 us  [select_facilities(): pl.pallas_call(kernel, out_shape=(jax.ShapeDtypeStruct((3, 1, BS), jnp.fl...]
    reshape x1 -> x0, local copies, waits for them, and re-layouts: 3.03 us -> none  [body(): both.reshape(2, 4, 4, 4, 4, 8, 4)]
    unnamed x1 -> x3, local copies, waits for them, and re-layouts: 0.74 us -> 3.28 us
where the time goes in v3:
time: 174 us
  Pallas kernels  161 us (93%)
  matrix products  4.79 us (3%)
  local copies, waits for them, and re-layouts  3.98 us (2%)
  other arithmetic  2.96 us (2%)
    pallas_call x1, Pallas kernels, select_facilities(): pl.pallas_call(kernel, out_shape=(jax.ShapeDtypeStruct((3, 1, BS), jnp.fl...  161 us
    dot_general x1, matrix products, body(): jnp.dot(table, sketches, preferred_element_type=jnp.float32)  4.79 us
  transfers between devices with their start and end apart: 1, of which 0 were waited for; matrix products, arithmetic and copies ran while one was open for 3% of the time, Pallas kernels for 0%

profile of v3, /device:TPU:9, one launch (start us, length us, event | category | flops | bytes accessed | tf_op | source)
XLA Modules:
  0.0 173.8 jit_solution(14861642492336804544)
XLA Ops:
  0.6 0.7 copy.20
  1.4 0.7 pad_add_fusion
  2.1 0.1 copy.22
  2.2 0.7 collective-permute-start
  2.9 0.7 fusion.1
  3.6 4.8 %convolution_convert_fusion.out_ref = bf16[512,4096]{1,0:T(8,128)(2,1)} fusion(bf16[256,4096]{1,0:T(8,128)(2,1)} %param.5, s32[256]{0:T(256)S(1)} %fusion.1), kind=kOutput, calls=%fused_computation | convolution fusion | flops 1075970048 | bytes 6292480 | tf_op jit(solution)/shard_map/dot_general | solution.py:526
  8.4 0.1 iota_add_fusion
  8.5 0.1 lt.88
  8.6 0.0 collective-permute-done
  8.7 0.1 fusion.3
  8.8 0.2 lt.90
  9.0 0.3 lt.91
  9.3 0.7 compare_convert_fusion.pick_ref
  10.0 0.6 compare_convert_fusion.1.valid_ref
  10.6 160.7 %facilities.1 = (f32[3,1,512]{2,1,0:T(1,128)}, f32[1,512]{1,0:T(1,128)}) custom-call(bf16[2,4,16,512]{3,2,1,0:T(8,128)(2,1)} %compare_convert_fusion.pick_ref, bf16[512,4096]{1,0:T(8,128)(2,1)} %convolution_convert_fusion.out_ref, f32[32,1,128]{2,1,0:T(1,128)} %compare_convert_fusion.1.valid_ref), custom_call_target="tpu_custom_call" | custom-call | tf_op jit(solution)/shard_map/facilities/pallas_call | solution.py:492
  171.3 1.3 copy.28
  172.6 1.3 copy.29
  (6 shorter events, 0.0 us)
Async XLA Ops:
  2.2 6.5 %collective-permute-start = (s32[16,128]{0,1:T(8,128)S(1)}, s32[16,128]{0,1:T(8,128)S(1)}, u32[]{:S(2)}, u32[]{:S(2)}) collective-permute-start(s32[16,128]{0,1:T(8,128)S(1)} %copy.22), channel_id=1, source_target_pairs={{0,1},{1,0},{2,3},{3,2},{4,5},{5,4},{6,7},{7,6},{8,9},{9,8},{10,11... | collective-permute-start | bytes 24584 | tf_op jit(solution)/shard_map/ppermute | solution.py:523

commit v4 on v3

--- a/solution.py
+++ b/solution.py
@@ -53,8 +53,8 @@
     return (v[0:8] + v[8:16]) + (v[16:24] + v[24:32])
 
 
-def kernel(pick_ref, out_ref, valid_ref, gain_ref, cover_ref, xs, relay0, relay1, relay2, gram, tab, hcol, a1col, a2col,
-           r1, r2, rg, sums, peak, part, got, final, pacc, landed, send1, recv1, send2, rstep, dsend, drecv, tsend, trecv, msend, mrecv):
+def kernel(pick_ref, out_ref, valid_ref, landed, xs, relay0, relay1, relay2, gram, tab, hcol, a1col, a2col,
+           r1, r2, sums, peak, part, got, final, pacc, send1, recv1, send2, rstep, dsend, drecv, tsend, trecv, msend, mrecv):
     x, y, z, core = my_coords()
     relays = (relay0, relay1, relay2)
     is_owner = x == (y + z) % 4
@@ -287,7 +287,12 @@
             tile(other, 3, 3, 17)
 
         wide = pacc[...]
+        mass = wide[3:4]
+        high = mass.astype(jnp.bfloat16).astype(jnp.float32)
+        middle = (mass - high).astype(jnp.bfloat16).astype(jnp.float32)
+        line = lax.broadcasted_iota(jnp.int32, (EXT, D), 0)
         hp = [0.5 * jnp.sum(wide[t : t + 1] * wide[t : t + 1], axis=1, keepdims=True) for t in range(3)]
+        wide = jnp.where(line == 3, high, jnp.where(line == 4, middle, jnp.where(line == 5, mass - high - middle, wide)))
         picked = wide.astype(jnp.bfloat16)
 
         eye = lax.broadcasted_iota(jnp.int32, (128, 128), 0) == lax.broadcasted_iota(jnp.int32, (128, 128), 1)
@@ -323,6 +328,7 @@
                 tab[core, r, 3:4, lanes] = p3
                 tab[core, r, 4:5, lanes] = h
                 tab[core, r, 5:6, lanes] = good[0:1]
+                tab[core, r, 6:7, lanes] = near[3:4, lanes] + near[4:5, lanes] + near[5:6, lanes]
 
         repeat(4, own_rows)
         sums[...] = jnp.zeros_like(sums)
@@ -349,7 +355,6 @@
             a2col[...] = column(tab[half, s, 2:3])
             r1[...] = jnp.zeros_like(r1)
             r2[...] = jnp.zeros_like(r2)
-            rg[...] = jnp.zeros_like(rg)
 
             def one_tile(r, carry):
                 slot = jnp.where(
@@ -365,31 +370,26 @@
                         a2u = tab[core, r, 2:3, lanes]
 
                         def strip(k, acc):
-                            c1, c2, cg, top = acc
+                            c1, c2, low = acc
                             at = pl.ds(pl.multiple_of(k * 32, 32), 32)
                             g = gram[slot, at, lanes]
-                            hq = hcol[at]
                             e = g - hu
-                            gap = hq - e
+                            f = g - hcol[at]
                             c1 = c1 + fold(jnp.maximum(e + a1col[at], 0.0))
                             c2 = c2 + fold(jnp.maximum(e + a2col[at], 0.0))
-                            cg = cg + fold(g)
-                            top = jnp.maximum(
-                                top, jnp.maximum(jnp.maximum(gap[0:8], gap[8:16]), jnp.maximum(gap[16:24], gap[24:32]))
+                            low = jnp.minimum(
+                                low, jnp.minimum(jnp.minimum(f[0:8], f[8:16]), jnp.minimum(f[16:24], f[24:32]))
                             )
                             if rows_too:
-                                f = g - hq
                                 r1[at] += jnp.maximum(f + a1u, 0.0)
                                 r2[at] += jnp.maximum(f + a2u, 0.0)
-                                rg[at] += g
-                            return c1, c2, cg, top
+                            return c1, c2, low
 
                         zero = jnp.zeros((8, 128), jnp.float32)
-                        c1, c2, cg, top = lax.fori_loop(0, BS // 32, strip, (zero, zero, zero, peak[...]), unroll=4)
+                        c1, c2, low = lax.fori_loop(0, BS // 32, strip, (zero, zero, zero + BIG), unroll=4)
                         sums[r, 0, :, lanes] += c1
                         sums[r, 1, :, lanes] += c2
-                        sums[r, 2, :, lanes] += cg
-                        peak[...] = top
+                        peak[...] = jnp.maximum(peak[...], hu - low)
 
                 @pl.when(diag)
                 def _():
@@ -403,7 +403,7 @@
 
             begin = jnp.where(jnp.logical_or(mine, s % 2 == core), s, s + 1)
             lax.fori_loop(begin, 4, one_tile, 0)
-            for n, acc in enumerate((r1, r2, rg)):
+            for n, acc in enumerate((r1, r2)):
                 part[half, s, n : n + 1] = jnp.sum(acc[...].T, axis=0, keepdims=True)
 
         repeat(8, row_block)
@@ -423,10 +423,10 @@
         bound = jnp.maximum(best, got[0, 3:4, 0:1]) * SCALE
 
         for r in range(4):
-            cols = [jnp.sum(sums[r, n], axis=0, keepdims=True) + part[core, r, n : n + 1] + got[r, n : n + 1] for n in range(3)]
+            cols = [jnp.sum(sums[r, n], axis=0, keepdims=True) + part[core, r, n : n + 1] + got[r, n : n + 1] for n in range(2)]
             h = tab[core, r, 4:5]
             ok = tab[core, r, 5:6] > 0.0
-            far = total * h + h_sum - cols[2]
+            far = total * h + h_sum - tab[core, r, 6:7]
             part[core, r, 4:5] = jnp.where(ok, (total * bound - far * SCALE) / total, 0.0)
             part[core, r, 5:6] = jnp.where(ok, cols[0] * SCALE / total, 0.0)
             part[core, r, 6:7] = jnp.where(ok, cols[1] * SCALE / total, 0.0)
@@ -446,7 +446,7 @@
                 final[m, :, pl.ds(pl.multiple_of(xx * 128, 128), 128)] += jnp.where(seat, spot, 0.0)[4:8]
 
         final[...] = jnp.zeros_like(final)
-        repeat(16, natural)
+        lax.fori_loop(0, 16, lambda n, carry: (natural(n), carry)[1], 0, unroll=4)
         me = lax.axis_index("dp")
         cls = lax.axis_index("cls")
         for m in range(8):
@@ -478,11 +478,6 @@
         @pl.when(jnp.logical_not(local))
         def _():
             pltpu.make_async_copy(landed.at[c], landed.at[c], mrecv.at[c]).wait()
-
-    rows = landed[0] + landed[1]
-    for t in range(3):
-        gain_ref[t] = rows[t : t + 1]
-    cover_ref[...] = rows[3:4]
 
 
 def select_facilities(outgoing, valid, pick):
@@ -491,22 +486,21 @@
     wide = pltpu.VMEM((BS, 128), jnp.float32)
     return pl.pallas_call(
         kernel,
-        out_shape=(jax.ShapeDtypeStruct((3, 1, BS), jnp.float32), jax.ShapeDtypeStruct((1, BS), jnp.float32)),
+        out_shape=jax.ShapeDtypeStruct((2, 4, BS), jnp.float32),
         in_specs=[vmem, pl.BlockSpec(memory_space=pl.ANY), vmem],
-        out_specs=(vmem, vmem),
+        out_specs=vmem,
         scratch_shapes=[pltpu.VMEM((2, 4, BS, D), jnp.bfloat16)]
         + [pltpu.VMEM((STEPS + STEPS // 2, UNIT, size), jnp.bfloat16) for _, size in PARTS]
         + [
             pltpu.VMEM((18, BS, BS), jnp.float32),
             pltpu.VMEM((2, 4, 8, BS), jnp.float32),
-            wide, wide, wide, wide, wide, wide,
-            pltpu.VMEM((4, 3, 8, BS), jnp.float32),
+            wide, wide, wide, wide, wide,
+            pltpu.VMEM((4, 2, 8, BS), jnp.float32),
             pltpu.VMEM((8, 128), jnp.float32),
             pltpu.VMEM((2, 4, 8, BS), jnp.float32),
             pltpu.VMEM((4, 8, BS), jnp.float32),
             pltpu.VMEM((8, 4, BS), jnp.float32),
             pltpu.VMEM((EXT, D), jnp.float32),
-            pltpu.VMEM((2, 4, BS), jnp.float32),
             sems((3, STEPS)), sems((3, STEPS + STEPS // 2)), sems((3, STEPS + STEPS // 2)), sems((STEPS,)),
             sems((5,)), sems((5,)), sems((2,)), sems((2,)), sems((8,)), sems((2,)),
         ],
@@ -534,11 +528,13 @@
     where = score * HALF + step * 128 + sx * UNIT + picked // 512 * 4 + picked % 4
     spot = jnp.pad(where, (0, EXT - 3), constant_values=-1)
     line = jnp.arange(4096, dtype=jnp.int32).reshape(8, 1, BS)
-    pick = (line == spot[None, :, None]).astype(jnp.bfloat16).reshape(2, 4, EXT, BS)
+    everyone = jnp.arange(EXT, dtype=jnp.int32)[None, :, None] == 3
+    pick = ((line == spot[None, :, None]) | everyone).astype(jnp.bfloat16).reshape(2, 4, EXT, BS)
     by_source = jnp.transpose(info[:8].reshape(8, 4, 4, 4, 2), (4, 1, 3, 2, 0))
     valid = (jnp.arange(4, dtype=jnp.int32) < by_source[..., None]).astype(jnp.float32).reshape(32, 1, 128)
 
-    return select_facilities(outgoing, valid, pick)
+    both = select_facilities(outgoing, valid, pick)
+    return (both[0, :3, None, :] + both[1, :3, None, :], both[0, 3:] + both[1, 3:])
 
 
 def solution(mesh):

time: 174 us -> 171 us (0.983)
  Pallas kernels: 161 us -> 157 us
  other arithmetic: 2.96 us -> 5.02 us
  local copies, waits for them, and re-layouts: 3.98 us -> 2.05 us
    pallas_call x1, Pallas kernels: 161 us -> 157 us  [select_facilities(): pl.pallas_call(kernel, out_shape=jax.ShapeDtypeStruct((2, 4, BS), jnp.flo...]
    add x0 -> x2, other arithmetic: none -> 2.02 us  [the longest x1 1.3 us: body(): both[0, 3:] + both[1, 3:]]
    unnamed x3 -> x2, local copies, waits for them, and re-layouts: 3.28 us -> 1.34 us
where the time goes in v4:
time: 171 us; the launch traced here: 170 us
  Pallas kernels  157 us (92%)
  other arithmetic  5.02 us (3%)
  matrix products  4.79 us (3%)
  local copies, waits for them, and re-layouts  2.05 us (1%)
    pallas_call x1, Pallas kernels, select_facilities(): pl.pallas_call(kernel, out_shape=jax.ShapeDtypeStruct((2, 4, BS), jnp.flo...  157 us
    dot_general x1, matrix products, body(): jnp.dot(table, sketches, preferred_element_type=jnp.float32)  4.79 us
  transfers between devices with their start and end apart: 1, of which 0 were waited for; matrix products, arithmetic and copies ran while one was open for 3% of the time, Pallas kernels for 0%

profile of v4, /device:TPU:9, one launch (start us, length us, event | category | flops | bytes accessed | tf_op | source)
XLA Modules:
  0.0 170.5 jit_solution(16252283624007668107)
XLA Ops:
  0.6 0.7 copy.24
  1.4 0.7 pad_add_fusion
  2.1 0.1 copy.26
  2.2 0.7 collective-permute-start
  2.9 0.1 iota_add_fusion
  3.0 0.7 fusion.1
  3.7 4.8 %convolution_convert_fusion.out_ref = bf16[512,4096]{1,0:T(8,128)(2,1)} fusion(bf16[256,4096]{1,0:T(8,128)(2,1)} %param.5, s32[256]{0:T(256)S(1)} %fusion.1), kind=kOutput, calls=%fused_computation | convolution fusion | flops 1075970048 | bytes 6292480 | tf_op jit(solution)/shard_map/dot_general | solution.py:520
  8.5 0.1 lt.88
  8.6 0.0 collective-permute-done
  8.7 0.1 fusion.3
  8.8 0.2 lt.90
  9.0 0.3 lt.91
  9.3 0.6 compare_convert_fusion.valid_ref
  9.9 0.8 or_convert_fusion.pick_ref
  10.7 157.2 %facilities.1 = f32[2,4,512]{2,1,0:T(4,128)} custom-call(bf16[2,4,16,512]{3,2,1,0:T(8,128)(2,1)} %or_convert_fusion.pick_ref, bf16[512,4096]{1,0:T(8,128)(2,1)} %convolution_convert_fusion.out_ref, f32[32,1,128]{2,1,0:T(1,128)} %compare_convert_fusion.valid_ref), custom_call_target="tpu_custom_call" | custom-call | tf_op jit(solution)/shard_map/facilities/pallas_call | solution.py:487
  167.9 1.3 add_bitcast_fusion.1
  169.2 0.7 add_bitcast_fusion
  169.9 0.6 copy.30
  (7 shorter events, 0.1 us)
Async XLA Ops:
  2.2 6.5 %collective-permute-start = (s32[16,128]{0,1:T(8,128)S(1)}, s32[16,128]{0,1:T(8,128)S(1)}, u32[]{:S(2)}, u32[]{:S(2)}) collective-permute-start(s32[16,128]{0,1:T(8,128)S(1)} %copy.26), channel_id=1, source_target_pairs={{0,1},{1,0},{2,3},{3,2},{4,5},{5,4},{6,7},{7,6},{8,9},{9,8},{10,11... | collective-permute-start | bytes 24584 | tf_op jit(solution)/shard_map/ppermute | solution.py:517

commit v5 on v4

--- a/solution.py
+++ b/solution.py
@@ -53,13 +53,48 @@
     return (v[0:8] + v[8:16]) + (v[16:24] + v[24:32])
 
 
-def kernel(pick_ref, out_ref, valid_ref, landed, xs, relay0, relay1, relay2, gram, tab, hcol, a1col, a2col,
-           r1, r2, sums, peak, part, got, final, pacc, send1, recv1, send2, rstep, dsend, drecv, tsend, trecv, msend, mrecv):
+def kernel(target_ref, sketch_ref, pick_ref, valid_ref, landed, xs, relay0, relay1, relay2, gram, tab, hcol, a1col, a2col,
+           r1, r2, sums, peak, part, got, final, pacc, send1, recv1, send2, rstep, dsend, drecv, tsend, trecv, msend, mrecv, load_sem, credit):
     x, y, z, core = my_coords()
     relays = (relay0, relay1, relay2)
     is_owner = x == (y + z) % 4
     partner = device_at(x, y, z, 1 - core)
     klass = class_at(y, z)
+    cls = lax.axis_index("cls")
+    other = 1 - core
+    out_ref = xs.at[other, 0]
+    load = pltpu.make_async_copy(sketch_ref, xs.at[other, 1, pl.ds(0, 256)], load_sem)
+    load.start()
+
+    barrier = pltpu.get_barrier_semaphore()
+
+    def greet(who):
+        pl.semaphore_signal(barrier, inc=1, device_id=who, device_id_type=MESH)
+
+    peers = [(a, b, c) for a in range(4) for b in range(4) for c in range(4) if 0 in (a, b, c) and (a, b, c) != (0, 0, 0)]
+    for a, b, c in peers:
+        greet(device_at((x + a) % 4, (y + b) % 4, (z + c) % 4, core))
+    greet(partner)
+    home_z = 2 * (cls % 2) + cls // 8
+    home_x = (y + home_z) % 4
+    for c in range(2):
+
+        @pl.when(jnp.logical_not(both_true(home_x == x, home_z == z, core == c)))
+        def _():
+            greet(device_at(home_x, y, home_z, c))
+
+    load.wait()
+    table = (lax.broadcasted_iota(jnp.int32, (512, 256), 0) == target_ref[...]).astype(jnp.bfloat16)
+
+    def place_slots(n):
+        lanes = pl.ds(pl.multiple_of(n * 512, 512), 512)
+        xs[other, 0, :, lanes] = jnp.dot(
+            table, xs[other, 1, 0:256, lanes], preferred_element_type=jnp.float32
+        ).astype(jnp.bfloat16)
+
+    repeat(8, place_slots)
+    members = jnp.where(cls == klass, 7, 8)
+    pl.semaphore_wait(barrier, len(peers) + 1 + jnp.where(is_owner, members, 0))
 
     def place_of(half, n, sx, start, size):
         return xs.at[half, n // 4, pl.ds(pl.multiple_of(n % 4 * 128 + sx * UNIT, UNIT), UNIT), pl.ds(start, size)]
@@ -119,10 +154,6 @@
                 def _():
                     bypass.start()
 
-                @pl.when(here)
-                def _():
-                    pltpu.make_async_copy(source, dest, rstep.at[n]).start()
-
     def line_owner(p):
         if p == 0:
             return (y + z) % 4, y, z
@@ -222,7 +253,13 @@
 
     @pl.when(is_owner)
     def _():
-        other = 1 - core
+        self_step = (4 - SKEW_Y) * x % 4 * 4 + (4 - SKEW_Z) * x % 4
+        xs[core, self_step // 4, pl.ds(pl.multiple_of(self_step % 4 * 128 + x * UNIT, UNIT), UNIT)] = xs[
+            other, 0, pl.ds(pl.multiple_of(klass * UNIT, UNIT), UNIT)
+        ]
+        repeat(STEPS, lambda n: sends(n, True))
+        pl.semaphore_signal(credit, inc=1, device_id=partner, device_id_type=MESH)
+        pl.semaphore_wait(credit, 1)
         pacc[...] = jnp.zeros_like(pacc)
 
         def take(half, r):
@@ -230,8 +267,13 @@
 
         def steps_in(r, first, count):
             for q in range(count):
-                rows = xs.at[core, r, pl.ds(pl.multiple_of((first + q) * 128, 128), 128)]
-                pltpu.make_async_copy(rows, rows, rstep.at[r * 4 + first + q]).wait()
+                n = r * 4 + first + q
+                for mine, count in ((False, 128), (True, 128 - UNIT)):
+                    rows = xs.at[core, r, pl.ds(pl.multiple_of((first + q) * 128, 128), count)]
+
+                    @pl.when((n == self_step) == mine)
+                    def _():
+                        pltpu.make_async_copy(rows, rows, rstep.at[n]).wait()
 
         def other_in(r):
             across(r).wait_recv()
@@ -448,7 +490,6 @@
         final[...] = jnp.zeros_like(final)
         lax.fori_loop(0, 16, lambda n, carry: (natural(n), carry)[1], 0, unroll=4)
         me = lax.axis_index("dp")
-        cls = lax.axis_index("cls")
         for m in range(8):
             local = jnp.logical_and(me == m, cls == klass)
 
@@ -470,8 +511,10 @@
         repeat(3, lambda r: across(r).wait_send())
         repeat(2, lambda h: across_half(h).wait_send())
 
-    repeat(STEPS, lambda n: sends(n, True))
-    cls = lax.axis_index("cls")
+    @pl.when(jnp.logical_not(is_owner))
+    def _():
+        repeat(STEPS, lambda n: sends(n, True))
+
     for c in range(2):
         local = both_true(is_owner, core == c, cls == klass)
 
@@ -480,14 +523,14 @@
             pltpu.make_async_copy(landed.at[c], landed.at[c], mrecv.at[c]).wait()
 
 
-def select_facilities(outgoing, valid, pick):
+def select_facilities(target, sketches, pick, valid):
     vmem = pl.BlockSpec(memory_space=pltpu.VMEM)
     sems = pltpu.SemaphoreType.DMA
     wide = pltpu.VMEM((BS, 128), jnp.float32)
     return pl.pallas_call(
         kernel,
         out_shape=jax.ShapeDtypeStruct((2, 4, BS), jnp.float32),
-        in_specs=[vmem, pl.BlockSpec(memory_space=pl.ANY), vmem],
+        in_specs=[vmem, pl.BlockSpec(memory_space=pl.ANY), vmem, vmem],
         out_specs=vmem,
         scratch_shapes=[pltpu.VMEM((2, 4, BS, D), jnp.bfloat16)]
         + [pltpu.VMEM((STEPS + STEPS // 2, UNIT, size), jnp.bfloat16) for _, size in PARTS]
@@ -503,21 +546,19 @@
             pltpu.VMEM((EXT, D), jnp.float32),
             sems((3, STEPS)), sems((3, STEPS + STEPS // 2)), sems((3, STEPS + STEPS // 2)), sems((STEPS,)),
             sems((5,)), sems((5,)), sems((2,)), sems((2,)), sems((8,)), sems((2,)),
+            sems, pltpu.SemaphoreType.REGULAR,
         ],
-        compiler_params=pltpu.CompilerParams(has_side_effects=True, vmem_limit_bytes=62 * 1024 * 1024),
+        compiler_params=pltpu.CompilerParams(collective_id=0, has_side_effects=True, vmem_limit_bytes=62 * 1024 * 1024),
         name="facilities",
-    )(pick, outgoing, valid)
+    )(target, sketches, pick, valid)
 
 
 def body(sketches, labels, places, counts, chosen):
     member = lax.axis_index("dp")
     cls = lax.axis_index("cls")
-    row_count = sketches.shape[0]
     info = jnp.concatenate([counts[0], jnp.pad(chosen[:, :1], ((0, 5), (0, 127)))], axis=0)
     swapped = lax.ppermute(info, "cls", [(n, n ^ 1) for n in range(16)])
     target = labels * UNIT + places // 512 * 4 + places % 4
-    table = (lax.broadcasted_iota(jnp.int32, (512, row_count), 0) == target[None, :]).astype(jnp.bfloat16)
-    outgoing = jnp.dot(table, sketches, preferred_element_type=jnp.float32).astype(jnp.bfloat16)
 
     x, y, z, core = member // 2, (cls // 2) % 4, (member % 2) * 2 + cls // 8, cls % 2
     info = jnp.where(core == z // 2, info, swapped)
@@ -533,7 +574,7 @@
     by_source = jnp.transpose(info[:8].reshape(8, 4, 4, 4, 2), (4, 1, 3, 2, 0))
     valid = (jnp.arange(4, dtype=jnp.int32) < by_source[..., None]).astype(jnp.float32).reshape(32, 1, 128)
 
-    both = select_facilities(outgoing, valid, pick)
+    both = select_facilities(target[None, :], sketches, pick, valid)
     return (both[0, :3, None, :] + both[1, :3, None, :], both[0, 3:] + both[1, 3:])
 
 

time: 171 us -> 162 us (0.947)
  Pallas kernels: 157 us -> 152 us
  matrix products: 4.79 us -> 0 us
    dot_general x1 -> x0, matrix products: 4.79 us -> none  [body(): jnp.dot(table, sketches, preferred_element_type=jnp.float32)]
    pallas_call x1, Pallas kernels: 157 us -> 152 us  [select_facilities(): pl.pallas_call(kernel, out_shape=jax.ShapeDtypeStruct((2, 4, BS), jnp.flo...]
  transfers between devices with their start and end apart: 1 -> 1, of which waited for: 0 -> 0; matrix products, arithmetic and copies ran while one was open for 3% -> 1% of each run, Pallas kernels for 0% -> 0%
where the time goes in v5:
time: 162 us
  Pallas kernels  152 us (94%)
  other arithmetic  5.57 us (3%)
  local copies, waits for them, and re-layouts  2.04 us (1%)
    pallas_call x1, Pallas kernels, select_facilities(): pl.pallas_call(kernel, out_shape=jax.ShapeDtypeStruct((2, 4, BS), jnp.flo...  152 us
  transfers between devices with their start and end apart: 1, of which 0 were waited for; matrix products, arithmetic and copies ran while one was open for 1% of the time, Pallas kernels for 0%

profile of v5, /device:TPU:9, one launch (start us, length us, event | category | flops | bytes accessed | tf_op | source)
XLA Modules:
  0.0 161.6 jit_solution(755062793946494066)
XLA Ops:
  0.6 0.7 copy.24
  1.4 0.7 pad_add_fusion
  2.1 0.1 copy.26
  2.2 0.7 collective-permute-start
  2.9 0.1 iota_add_fusion
  3.0 1.3 fusion
  4.3 0.1 lt.88
  4.4 0.0 collective-permute-done
  4.5 0.2 lt.90
  4.7 0.3 lt.91
  4.9 0.1 fusion.2
  5.1 0.6 compare_convert_fusion.valid_ref
  5.7 0.8 or_convert_fusion.pick_ref
  6.5 152.5 %facilities.1 = f32[2,4,512]{2,1,0:T(4,128)} custom-call(s32[1,256]{1,0:T(1,128)} %bitcast.21, bf16[256,4096]{1,0:T(8,128)(2,1)} %sketch_ref.1, bf16[2,4,16,512]{3,2,1,0:T(8,128)(2,1)} %or_convert_fusion.pick_ref, f32[32,1,128]{2,1,0:T(1,128)} %compare_convert_fusion.valid_ref), custom_call_target="tpu_custom_call" | custom-call | tf_op jit(solution)/shard_map/facilities/pallas_call | solution.py:530
  158.9 0.7 add_bitcast_fusion
  159.7 1.3 add_bitcast_fusion.1
  161.0 0.6 copy.30
  (7 shorter events, 0.1 us)
Async XLA Ops:
  2.2 2.2 %collective-permute-start = (s32[16,128]{0,1:T(8,128)S(1)}, s32[16,128]{0,1:T(8,128)S(1)}, u32[]{:S(2)}, u32[]{:S(2)}) collective-permute-start(s32[16,128]{0,1:T(8,128)S(1)} %copy.26), channel_id=1, source_target_pairs={{0,1},{1,0},{2,3},{3,2},{4,5},{5,4},{6,7},{7,6},{8,9},{9,8},{10,11... | collective-permute-start | bytes 24584 | tf_op jit(solution)/shard_map/ppermute | solution.py:560

commit v6 on v5

--- a/solution.py
+++ b/solution.py
@@ -9,7 +9,7 @@
 D = 4096
 BIG = 1e30
 SCALE = 2.0 / D
-PARTS = ((0, 1408), (1408, 1408), (2816, 1280))
+PARTS = ((0, 1280), (1280, 1408), (2688, 1408))
 UNIT = 32
 STEPS = 16
 BS = 512
@@ -428,7 +428,7 @@
                             return c1, c2, low
 
                         zero = jnp.zeros((8, 128), jnp.float32)
-                        c1, c2, low = lax.fori_loop(0, BS // 32, strip, (zero, zero, zero + BIG), unroll=4)
+                        c1, c2, low = lax.fori_loop(0, BS // 32, strip, (zero, zero, zero + BIG), unroll=8)
                         sums[r, 0, :, lanes] += c1
                         sums[r, 1, :, lanes] += c2
                         peak[...] = jnp.maximum(peak[...], hu - low)
@@ -488,7 +488,7 @@
                 final[m, :, pl.ds(pl.multiple_of(xx * 128, 128), 128)] += jnp.where(seat, spot, 0.0)[4:8]
 
         final[...] = jnp.zeros_like(final)
-        lax.fori_loop(0, 16, lambda n, carry: (natural(n), carry)[1], 0, unroll=4)
+        lax.fori_loop(0, 16, lambda n, carry: (natural(n), carry)[1], 0, unroll=8)
         me = lax.axis_index("dp")
         for m in range(8):
             local = jnp.logical_and(me == m, cls == klass)
@@ -556,13 +556,15 @@
 def body(sketches, labels, places, counts, chosen):
     member = lax.axis_index("dp")
     cls = lax.axis_index("cls")
-    info = jnp.concatenate([counts[0], jnp.pad(chosen[:, :1], ((0, 5), (0, 127)))], axis=0)
-    swapped = lax.ppermute(info, "cls", [(n, n ^ 1) for n in range(16)])
+    pairs = [(n, n ^ 1) for n in range(16)]
+    counts_there = lax.ppermute(counts, "cls", pairs)
+    chosen_there = lax.ppermute(chosen, "cls", pairs)
     target = labels * UNIT + places // 512 * 4 + places % 4
 
     x, y, z, core = member // 2, (cls // 2) % 4, (member % 2) * 2 + cls // 8, cls % 2
-    info = jnp.where(core == z // 2, info, swapped)
-    picked = info[8:11, 0]
+    ours = core == z // 2
+    picked = jnp.where(ours, chosen, chosen_there)[:, 0]
+    class_counts = jnp.where(ours, counts, counts_there)[0]
     source = picked % 512 // 4
     sx, sz, sy, score = source // 32, source // 8 % 4, source // 2 % 4, source % 2
     step = (sy - y - SKEW_Y * sx + 16) % 4 * 4 + (sz - z - SKEW_Z * sx + 16) % 4
@@ -571,7 +573,7 @@
     line = jnp.arange(4096, dtype=jnp.int32).reshape(8, 1, BS)
     everyone = jnp.arange(EXT, dtype=jnp.int32)[None, :, None] == 3
     pick = ((line == spot[None, :, None]) | everyone).astype(jnp.bfloat16).reshape(2, 4, EXT, BS)
-    by_source = jnp.transpose(info[:8].reshape(8, 4, 4, 4, 2), (4, 1, 3, 2, 0))
+    by_source = jnp.transpose(class_counts.reshape(8, 4, 4, 4, 2), (4, 1, 3, 2, 0))
     valid = (jnp.arange(4, dtype=jnp.int32) < by_source[..., None]).astype(jnp.float32).reshape(32, 1, 128)
 
     both = select_facilities(target[None, :], sketches, pick, valid)

time: 162 us -> 160 us (0.988)
  transfers between devices with their start and end apart: 1 -> 2, of which waited for: 0 -> 0; matrix products, arithmetic and copies ran while one was open for 1% -> 1% of each run, Pallas kernels for 0% -> 0%
where the time goes in v6:
time: 160 us
  Pallas kernels  151 us (94%)
  other arithmetic  4.8 us (3%)
  local copies, waits for them, and re-layouts  1.99 us (1%)
    pallas_call x1, Pallas kernels, select_facilities(): pl.pallas_call(kernel, out_shape=jax.ShapeDtypeStruct((2, 4, BS), jnp.flo...  151 us
  transfers between devices with their start and end apart: 2, of which 0 were waited for; matrix products, arithmetic and copies ran while one was open for 1% of the time, Pallas kernels for 0%

profile of v6, /device:TPU:9, one launch (start us, length us, event | category | flops | bytes accessed | tf_op | source)
XLA Modules:
  0.0 159.6 jit_solution(3105460897861256014)
XLA Ops:
  0.6 0.8 copy.15
  1.4 0.7 collective-permute-start.1
  2.2 0.1 collective-permute-start
  2.3 0.1 lt.88
  2.4 0.1 iota_add_fusion
  2.5 1.3 fusion
  3.8 0.0 collective-permute-done
  3.8 0.1 fusion.2
  3.8 0.7 or_convert_fusion.pick_ref
  4.6 0.0 collective-permute-done.1
  4.6 0.2 lt.90
  4.8 0.3 lt.91
  5.1 0.6 compare_convert_fusion.valid_ref
  5.7 151.3 %facilities.1 = f32[2,4,512]{2,1,0:T(4,128)} custom-call(s32[1,256]{1,0:T(1,128)} %bitcast.19, bf16[256,4096]{1,0:T(8,128)(2,1)} %sketch_ref.1, bf16[2,4,16,512]{3,2,1,0:T(8,128)(2,1)} %or_convert_fusion.pick_ref, f32[32,1,128]{2,1,0:T(1,128)} %compare_convert_fusion.valid_ref), custom_call_target="tpu_custom_call" | custom-call | tf_op jit(solution)/shard_map/facilities/pallas_call | solution.py:530
  157.0 0.7 add_bitcast_fusion
  157.7 1.3 add_bitcast_fusion.1
  159.0 0.6 copy.19
  (7 shorter events, 0.1 us)
Async XLA Ops:
  1.4 3.2 %collective-permute-start.1 = (s32[1,8,128]{1,2,0:T(8,128)S(1)}, s32[1,8,128]{1,2,0:T(8,128)S(1)}, u32[]{:S(2)}, u32[]{:S(2)}) collective-permute-start(s32[1,8,128]{1,2,0:T(8,128)S(1)} %copy.15), channel_id=1, source_target_pairs={{0,1},{1,0},{2,3},{3,2},{4,5},{5,4},{6,7},{7,6},{8,9},{9,8},{10,11... | collective-permute-start | bytes 12296 | tf_op jit(solution)/shard_map/ppermute | solution.py:560
  2.2 1.6 collective-permute-start

commit v7 on v6

--- a/solution.py
+++ b/solution.py
@@ -372,7 +372,7 @@
                 tab[core, r, 5:6, lanes] = good[0:1]
                 tab[core, r, 6:7, lanes] = near[3:4, lanes] + near[4:5, lanes] + near[5:6, lanes]
 
-        repeat(4, own_rows)
+        lax.fori_loop(0, 4, lambda r, carry: (own_rows(r), carry)[1], 0, unroll=4)
         sums[...] = jnp.zeros_like(sums)
         peak[...] = jnp.zeros_like(peak)
         tables = pltpu.make_async_remote_copy(
@@ -428,7 +428,7 @@
                             return c1, c2, low
 
                         zero = jnp.zeros((8, 128), jnp.float32)
-                        c1, c2, low = lax.fori_loop(0, BS // 32, strip, (zero, zero, zero + BIG), unroll=8)
+                        c1, c2, low = lax.fori_loop(0, BS // 32, strip, (zero, zero, zero + BIG), unroll=16)
                         sums[r, 0, :, lanes] += c1
                         sums[r, 1, :, lanes] += c2
                         peak[...] = jnp.maximum(peak[...], hu - low)

time: 160 us -> 158 us (0.988)
  Pallas kernels: 151 us -> 149 us
    pallas_call x1, Pallas kernels: 151 us -> 149 us  [select_facilities(): pl.pallas_call(kernel, out_shape=jax.ShapeDtypeStruct((2, 4, BS), jnp.flo...]
where the time goes in v7:
time: 158 us
  Pallas kernels  149 us (94%)
  other arithmetic  4.8 us (3%)
  local copies, waits for them, and re-layouts  1.99 us (1%)
    pallas_call x1, Pallas kernels, select_facilities(): pl.pallas_call(kernel, out_shape=jax.ShapeDtypeStruct((2, 4, BS), jnp.flo...  149 us
  transfers between devices with their start and end apart: 2, of which 0 were waited for; matrix products, arithmetic and copies ran while one was open for 1% of the time, Pallas kernels for 0%

profile of v7, /device:TPU:9, one launch (start us, length us, event | category | flops | bytes accessed | tf_op | source)
XLA Modules:
  0.0 157.8 jit_solution(8809579574688788045)
XLA Ops:
  0.6 0.8 copy.15
  1.4 0.7 collective-permute-start.1
  2.2 0.1 collective-permute-start
  2.3 0.1 lt.88
  2.4 0.1 iota_add_fusion
  2.5 1.3 fusion
  3.8 0.0 collective-permute-done
  3.8 0.1 fusion.2
  3.8 0.7 or_convert_fusion.pick_ref
  4.6 0.0 collective-permute-done.1
  4.6 0.2 lt.90
  4.8 0.3 lt.91
  5.1 0.6 compare_convert_fusion.valid_ref
  5.7 149.4 %facilities.1 = f32[2,4,512]{2,1,0:T(4,128)} custom-call(s32[1,256]{1,0:T(1,128)} %bitcast.19, bf16[256,4096]{1,0:T(8,128)(2,1)} %sketch_ref.1, bf16[2,4,16,512]{3,2,1,0:T(8,128)(2,1)} %or_convert_fusion.pick_ref, f32[32,1,128]{2,1,0:T(1,128)} %compare_convert_fusion.valid_ref), custom_call_target="tpu_custom_call" | custom-call | tf_op jit(solution)/shard_map/facilities/pallas_call | solution.py:530
  155.2 0.7 add_bitcast_fusion
  155.9 1.3 add_bitcast_fusion.1
  157.2 0.6 copy.19
  (7 shorter events, 0.1 us)
Async XLA Ops:
  1.4 3.2 %collective-permute-start.1 = (s32[1,8,128]{1,2,0:T(8,128)S(1)}, s32[1,8,128]{1,2,0:T(8,128)S(1)}, u32[]{:S(2)}, u32[]{:S(2)}) collective-permute-start(s32[1,8,128]{1,2,0:T(8,128)S(1)} %copy.15), channel_id=1, source_target_pairs={{0,1},{1,0},{2,3},{3,2},{4,5},{5,4},{6,7},{7,6},{8,9},{9,8},{10,11... | collective-permute-start | bytes 12296 | tf_op jit(solution)/shard_map/ppermute | solution.py:560
  2.2 1.6 %collective-permute-start = (s32[3,1]{0,1:T(1,128)}, s32[3,1]{0,1:T(1,128)S(1)}, u32[]{:S(2)}, u32[]{:S(2)}) collective-permute-start(s32[3,1]{0,1:T(1,128)} %param.9), channel_id=1, source_target_pairs={{0,1},{1,0},{2,3},{3,2},{4,5},{5,4},{6,7},{7,6},{8,9},{9,8},{10,11... | collective-permute-start | bytes 44 | tf_op jit(solution)/shard_map/ppermute | solution.py:561
